TPU v7x, 32 devices: a whole 2x2x4 slice. The times are simulated.
32 devices in a mesh: seq: 4 (over y, x), fsdp: 8 (over z, core).
Axes of the slice: x: 2, y: 2, z: 4, core: 2. Of those that a mesh axis runs over, the one named last changes fastest.
Arguments:
- tokens: bfloat16 [8, 1024, 1536], P('fsdp', 'seq'), may hold values from -6 to 6
- input_projection_weight: bfloat16 [1536, 6448], P('fsdp'), may hold values from -0.15625 to 0.15625
- pre_gain: bfloat16 [1536], P('fsdp'), may hold values from 0.25 to 1.75
- conv_weight: bfloat16 [3328, 4], P('fsdp'), may hold values from -3 to 3
- conv_bias: bfloat16 [3328], P('fsdp'), may hold values from -0.5 to 0.5
- step_bias: bfloat16 [48], P('fsdp'), may hold values from -6 to -1
- decay_log: bfloat16 [48], P('fsdp'), may hold values from 0 to 2.765625
- skip_gain: bfloat16 [48], P('fsdp'), may hold values from 0.5 to 1.5
- post_gain: bfloat16 [3072], P('fsdp'), may hold values from 0.25 to 1.75
- output_projection_weight: bfloat16 [3072, 1536], P(None, 'fsdp'), may hold values from -0.109375 to 0.109375
- cotangent: bfloat16 [8, 1024, 1536], P('fsdp', 'seq'), may hold values from -6 to 6
Outputs:
- block_out: float32 [8, 1024, 1536], P('fsdp', 'seq')
- grad_tokens: float32 [8, 1024, 1536], P('fsdp', 'seq')
- grad_in_weight: float32 [1536, 6448], P('fsdp')
- grad_pre_gain: float32 [1536], P('fsdp')
- grad_conv_weight: float32 [3328, 4], P('fsdp')
- grad_conv_bias: float32 [3328], P('fsdp')
- grad_step_bias: float32 [48], P('fsdp')
- grad_decay_log: float32 [48], P('fsdp')
- grad_skip_gain: float32 [48], P('fsdp')
- grad_post_gain: float32 [3072], P('fsdp')
- grad_out_weight: float32 [3072, 1536], P(None, 'fsdp')
All inputs are finite; a program needn't handle non-finite values.
Results may differ from a plain program's by a relative error of at most 0.012.
The roundings to bfloat16 on the way count: a program that leaves them out, or rounds other values in their place, can miss the bound.
Values may be sent and summed in bfloat16 or wider, within the bound.
A program may use at most 256 MiB of HBM per device.

v0:
```python
import functools

import jax
import jax.numpy as jnp
from jax import lax
from jax.experimental import pallas as pl
from jax.experimental.pallas import tpu as pltpu
from jax.sharding import PartitionSpec as P

D = 1536
INNER = 3072
STATE = 128
HEADS = 48
XBC = INNER + 2 * STATE
EPS = 1e-05

SEQ = 4
W = INNER // SEQ
HL = HEADS // SEQ
HW = INNER // HEADS
CH = W + 2 * STATE
VC = CH + 128
Q = 128

F32 = jnp.float32
BF16 = jnp.bfloat16
MESH = pl.DeviceIdType.MESH
HIGH = lax.Precision.HIGHEST
VMEM = pl.BlockSpec(memory_space=pltpu.VMEM)
ANY = pl.BlockSpec(memory_space=pl.ANY)
VMEM_LIMIT = 64000 * 1024


def rcopy(src, dst, send_sem, recv_sem, device):
    return pltpu.make_async_remote_copy(
        src_ref=src, dst_ref=dst, send_sem=send_sem, recv_sem=recv_sem, device_id=device, device_id_type=MESH
    )


def signal(sem, device):
    pl.semaphore_signal(sem, inc=1, device_id=device, device_id_type=MESH)


def nn(a, b, precision=None):
    return lax.dot_general(a, b, (((1,), (0,)), ((), ())), precision=precision, preferred_element_type=F32)


def nt(a, b, precision=None):
    return lax.dot_general(a, b, (((1,), (1,)), ((), ())), precision=precision, preferred_element_type=F32)


def seq_gather_start(refs, outs, send, recv, px, py, me):
    for g, (src, out) in enumerate(zip(refs, outs)):
        n = src.shape[0]
        own = out.at[pl.ds(me * n, n)]
        rcopy(src, own, send.at[g, 0], recv.at[g, 0], {"seq": px}).start()
        rcopy(src, own, send.at[g, 1], recv.at[g, 1], {"seq": py}).start()


def seq_gather_relay(g, src, out, send, recv, px, py, me):
    n = src.shape[0]
    h = n // 2
    own = out.at[pl.ds(me * n, n)]
    rcopy(src, own, send.at[g, 0], recv.at[g, 0], {"seq": px}).wait_recv()
    top = out.at[pl.ds(px * n, h)]
    rcopy(top, top, send.at[g, 2], recv.at[g, 2], {"seq": py}).start()
    rcopy(src, own, send.at[g, 1], recv.at[g, 1], {"seq": py}).wait_recv()
    low = out.at[pl.ds(py * n + h, h)]
    rcopy(low, low, send.at[g, 3], recv.at[g, 3], {"seq": px}).start()


def seq_gather_finish(g, src, out, send, recv, px, py, me):
    n = src.shape[0]
    h = n // 2
    own = out.at[pl.ds(me * n, n)]
    half = out.at[pl.ds(me * n, h)]
    rcopy(half, half, send.at[g, 2], recv.at[g, 2], {"seq": py}).wait()
    rcopy(half, half, send.at[g, 3], recv.at[g, 3], {"seq": px}).wait()
    rcopy(src, own, send.at[g, 0], recv.at[g, 0], {"seq": px}).wait_send()
    rcopy(src, own, send.at[g, 1], recv.at[g, 1], {"seq": py}).wait_send()


def softplus(x):
    return jnp.maximum(x, 0.0) + jnp.log1p(jnp.exp(-jnp.abs(x)))


def sigmoid(x):
    return 1.0 / (1.0 + jnp.exp(-x))


def rates_of(r_ref, rows, hp_ref, tri):
    raw = r_ref[rows, :].astype(F32) + hp_ref[0:1, :]
    dt = softplus(raw)
    lam = nn(tri, dt * hp_ref[1:2, :], HIGH)
    return raw, dt, lam


def spread(mat, h):
    return jnp.broadcast_to(mat[:, h : h + 1], (mat.shape[0], 128))


def scan_fwd_blocks(
    v_ref, s_ref, r_ref, kw_ref, hp_ref, ex_ref, mixed_ref, st_ref, buf, hst, xw_s, er_s, between
):
    blocks = v_ref.shape[0] // Q
    row = lax.broadcasted_iota(jnp.int32, (Q, Q), 0)
    col = lax.broadcasted_iota(jnp.int32, (Q, Q), 1)
    causal = row >= col
    tri = causal.astype(F32)
    low = lax.broadcasted_iota(jnp.int32, (Q, 128), 1) < HW
    low1 = lax.broadcasted_iota(jnp.int32, (1, 128), 1) < HW
    buf[0:8, :] = jnp.zeros((8, CH), F32)
    hst[...] = jnp.zeros_like(hst)

    def block(b, carry):
        rows = pl.ds(pl.multiple_of(b * Q, Q), Q)
        buf[8 : 8 + Q, 0:W] = v_ref[rows, :].astype(F32)
        buf[8 : 8 + Q, W:CH] = s_ref[rows, :].astype(F32)
        k = kw_ref[4:5, :] + buf[5 : 5 + Q, :] * kw_ref[0:1, :]
        for j in range(1, 4):
            k = k + buf[5 + j : 5 + j + Q, :] * kw_ref[j : j + 1, :]
        buf[0:8, :] = buf[Q : Q + 8, :]
        x = k * sigmoid(k)
        bs, cs = x[:, W : W + STATE], x[:, W + STATE :]
        _, dt, lam = rates_of(r_ref, rows, hp_ref, tri)
        lam_t, dt_t = lam.T, dt.T
        last = lam[Q - 1 : Q, :]
        tail = dt * jnp.exp(last - lam)
        aff = nt(cs, bs, HIGH)
        st_ref[b] = hst[...].astype(BF16)
        ch = nn(cs.astype(BF16), st_ref[b])
        for i in range(HL // 2):
            at = slice(128 * i, 128 * i + 128)
            xp = x[:, at]
            xb = xp.astype(BF16)
            y, lc = [], []
            for h in (2 * i, 2 * i + 1):
                lcol = spread(lam, h)
                within = jnp.exp(jnp.where(causal, lcol - lam_t[h : h + 1, :], -1e30))
                y.append(nn((aff * within * dt_t[h : h + 1, :]).astype(BF16), xb))
                lc.append(lcol)
            out = jnp.where(low, y[0], y[1])
            out = out + jnp.exp(jnp.where(low, lc[0], lc[1])) * ch[:, at] + ex_ref[0:1, at] * xp
            mixed_ref[rows, at] = out.astype(BF16)
            xw_s[:, at] = (xp * jnp.where(low, spread(tail, 2 * i), spread(tail, 2 * i + 1))).astype(BF16)
            er_s[0:1, at] = jnp.exp(jnp.where(low1, spread(last, 2 * i), spread(last, 2 * i + 1)))
        hst[...] = hst[...] * er_s[0:1, :] + nn(bs.T.astype(BF16), xw_s[...])
        between(b)
        return carry

    lax.fori_loop(0, blocks, block, 0)


def scan_bwd_blocks(
    v_ref, s_ref, r_ref, dy_ref, st_ref, kw_ref, hp_ref, ex_ref,
    dv_ref, gcw_ref, gch_ref, ghd_ref,
    buf, cbuf, dhst, rowp, xw_s, e_s, er_s, between,
):
    blocks = v_ref.shape[0] // Q
    row = lax.broadcasted_iota(jnp.int32, (Q, Q), 0)
    col = lax.broadcasted_iota(jnp.int32, (Q, Q), 1)
    tri = (row >= col).astype(F32)
    later = col >= row
    suffix = later.astype(F32)
    strict = (col < row).astype(F32)
    lane = lax.broadcasted_iota(jnp.int32, (Q, 128), 1)
    lane1 = lax.broadcasted_iota(jnp.int32, (1, 128), 1)
    low = lane < HW
    low1 = lane1 < HW
    buf[Q : Q + 8, :] = jnp.zeros((8, CH), F32)
    dhst[...] = jnp.zeros_like(dhst)
    rowp[...] = jnp.zeros_like(rowp)
    gcw_ref[...] = jnp.zeros_like(gcw_ref)
    gch_ref[...] = jnp.zeros_like(gch_ref)
    ghd_ref[...] = jnp.zeros_like(ghd_ref)

    def block(i0, carry):
        b = blocks - 1 - i0
        rows = pl.ds(pl.multiple_of(b * Q, Q), Q)
        before = pl.ds(pl.multiple_of(jnp.maximum(b * Q - 16, 0), 16), 16)
        keep = (b > 0).astype(F32)
        cbuf[0:8, 0:W] = v_ref[before, :].astype(F32)[8:16, :] * keep
        cbuf[0:8, W:CH] = s_ref[before, :].astype(F32)[8:16, :] * keep
        cbuf[8 : 8 + Q, 0:W] = v_ref[rows, :].astype(F32)
        cbuf[8 : 8 + Q, W:CH] = s_ref[rows, :].astype(F32)
        k = kw_ref[4:5, :] + cbuf[5 : 5 + Q, :] * kw_ref[0:1, :]
        for j in range(1, 4):
            k = k + cbuf[5 + j : 5 + j + Q, :] * kw_ref[j : j + 1, :]
        sg = sigmoid(k)
        x = k * sg
        ds = sg * (1.0 + k * (1.0 - sg))
        bs, cs = x[:, W : W + STATE], x[:, W + STATE :]
        bb, cb = bs.astype(BF16), cs.astype(BF16)
        raw, dt, lam = rates_of(r_ref, rows, hp_ref, tri)
        lam_t = lam.T
        last = lam[Q - 1 : Q, :]
        aff_t = nt(bs, cs, HIGH)
        hb = st_ref[b]
        dhb = dhst[...].astype(BF16)
        ch = nn(cb, hb)
        bd = nn(bb, dhb)
        daff_t = jnp.zeros((Q, Q), F32)
        col_n = jnp.zeros((Q, 128), F32)
        col_i = jnp.zeros((Q, 128), F32)
        row_i = jnp.zeros((Q, 128), F32)
        through = jnp.zeros((1, 128), F32)
        for i in range(HL // 2):
            at = slice(128 * i, 128 * i + 128)
            xp = x[:, at]
            xb = xp.astype(BF16)
            dyb = dy_ref[rows, at]
            dyf = dyb.astype(F32)
            z, lc, dc = [], [], []
            for h in (2 * i, 2 * i + 1):
                mine = low if h % 2 == 0 else jnp.logical_not(low)
                lcol, dcol = spread(lam, h), spread(dt, h)
                within = jnp.exp(jnp.where(later, lam_t[h : h + 1, :] - lcol, -1e30))
                g = nt(jnp.where(mine, xp, 0.0).astype(BF16), dyb)
                lg = within * g
                lgd = lg * dcol
                daff_t = daff_t + lgd
                col_n = jnp.where(lane == h, jnp.sum(aff_t * lg, axis=1, keepdims=True), col_n)
                rowp[h : h + 1, :] = jnp.sum(aff_t * lgd, axis=0, keepdims=True)
                z.append(nn((aff_t * within).astype(BF16), dyb))
                lc.append(lcol)
                dc.append(dcol)
            lamp = jnp.where(low, lc[0], lc[1])
            dtp = jnp.where(low, dc[0], dc[1])
            lastp = jnp.where(low1, spread(last, 2 * i), spread(last, 2 * i + 1))
            e = dyf * jnp.exp(lamp)
            e_s[:, at] = e.astype(BF16)
            ew = jnp.exp(lastp - lamp)
            bdp = bd[:, at]
            xw_s[:, at] = (xp * (dtp * ew)).astype(BF16)
            er_s[0:1, at] = jnp.exp(lastp)
            re = e * ch[:, at]
            ci = xp * bdp * ew
            th = jnp.sum(dhst[:, at] * hb[:, at].astype(F32), axis=0, keepdims=True) * er_s[0:1, at]
            for h in (2 * i, 2 * i + 1):
                mine = low if h % 2 == 0 else jnp.logical_not(low)
                mine1 = low1 if h % 2 == 0 else jnp.logical_not(low1)
                row_i = jnp.where(lane == h, jnp.sum(jnp.where(mine, re, 0.0), axis=1, keepdims=True), row_i)
                col_i = jnp.where(lane == h, jnp.sum(jnp.where(mine, ci, 0.0), axis=1, keepdims=True), col_i)
                through = jnp.where(
                    lane1 == h, jnp.sum(jnp.where(mine1, th, 0.0), axis=1, keepdims=True), through
                )
            dx = dtp * jnp.where(low, z[0], z[1]) + bdp * (dtp * ew) + ex_ref[0:1, at] * dyf
            gch_ref[0:1, at] += jnp.sum(dyf * xp, axis=0, keepdims=True)
            buf[0:Q, at] = dx * ds[:, at]
        daff_b = daff_t.astype(BF16)
        d_bs = nt(xw_s[...], dhb) + nn(daff_b, cb)
        d_cs = nt(e_s[...], hb) + nn(daff_t.T.astype(BF16), bb)
        buf[0:Q, W : W + STATE] = d_bs * ds[:, W : W + STATE]
        buf[0:Q, W + STATE : CH] = d_cs * ds[:, W + STATE :]
        dhst[...] = dhst[...] * er_s[0:1, :] + nn(cs.T.astype(BF16), e_s[...])
        after = nn(suffix, rowp[...].T - dt * col_n + row_i, HIGH) + nn(strict, dt * col_i, HIGH) + through
        d_rate = (col_n + col_i + hp_ref[1:2, :] * after) * sigmoid(raw)
        ghd_ref[0:1, :] += jnp.sum(d_rate, axis=0, keepdims=True)
        ghd_ref[1:2, :] += jnp.sum(dt * after, axis=0, keepdims=True) * hp_ref[1:2, :]
        dv_ref[rows, CH:VC] = d_rate.astype(BF16)
        for at in (slice(0, W), slice(W, CH)):
            raw_v = cbuf[8 : 8 + Q, at]
            dk = buf[0:Q, at]
            dv = dk * kw_ref[3:4, at]
            gcw_ref[4:5, at] += jnp.sum(dk, axis=0, keepdims=True)
            gcw_ref[3:4, at] += jnp.sum(dk * raw_v, axis=0, keepdims=True)
            for j in range(3):
                dk = buf[3 - j : 3 - j + Q, at]
                dv = dv + dk * kw_ref[j : j + 1, at]
                gcw_ref[j : j + 1, at] += jnp.sum(dk * raw_v, axis=0, keepdims=True)
            dv_ref[rows, at] = dv.astype(BF16)
        buf[Q : Q + 8, :] = buf[0:8, :]
        between(i0)
        return carry

    lax.fori_loop(0, blocks, block, 0)


GROUPS = 4


def place(block, at, width):
    start, shift = at // 128 * 128, at % 128
    lanes = -(-(width + shift) // 128) * 128
    have = block.shape[1]
    if lanes > have:
        block = jnp.concatenate([block, jnp.zeros((block.shape[0], lanes - have), block.dtype)], axis=1)
    else:
        block = block[:, :lanes]
    if shift:
        block = pltpu.roll(block, shift, 1)
    return start, lanes, block


def front_kernel(
    nf, tok, cot, win, wst, wout, small,
    x_out, cot_out, nrm_out, wv_out, ws_out, wg_out, wo_out, mix_out, gate_out, mixed_out, st_out, dsh_out,
    kw_s, hp_s, ex_s, pre_s, stat_s,
    x_s, cot_s, nrm_s, wv_s, ws_s, wg_s, wo_s, mix_s, gate_s, mixed_s, st_s, dsh_s,
    small_s, conv_s, post_s, stat_own, stat_got,
    buf, hst, xw_s, er_s,
    xs, xr, zs, zr, ms, mr, es, er, ls, os_,
):
    s = lax.axis_index("seq")
    f = lax.axis_index("fsdp")
    px, py = s ^ 1, s ^ 2
    nl = nf // 2
    p, c = f // 2, f % 2
    partner = p * 2 + 1 - c
    bar = pltpu.get_barrier_semaphore()
    for k in range(1, SEQ):
        signal(bar, {"seq": s ^ k})
    for k in range(1, nf):
        signal(bar, {"fsdp": lax.rem(f + k, nf)})
    pl.semaphore_wait(bar, nf - 1 + SEQ - 1)

    n = win.shape[0]
    rows = tok.shape[0]
    length = rows * SEQ
    ins = (
        win.at[:, pl.ds(pl.multiple_of(INNER + s * W, 128), W)],
        wst,
        win.at[:, pl.ds(pl.multiple_of(s * W, 128), W)],
        wout,
    )
    outs = (wv_s, ws_s, wg_s, wo_s)

    def row(g, i):
        return outs[g].at[pl.ds(i * n, n)]

    def hop(g, src, i, way, k, device):
        return rcopy(src, row(g, i), zs.at[g, way, k], zr.at[g, i], {"fsdp": device})

    def own_send(g):
        @pl.when(p < nl - 1)
        def _():
            hop(g, ins[g], f, 0, 0, f + 2).start()

        @pl.when(p > 0)
        def _():
            hop(g, ins[g], f, 1, 0, f - 2).start()

        hop(g, ins[g], f, 2, 0, partner).start()
        pltpu.make_async_copy(ins[g], row(g, f), ls.at[g]).start()

    def step(g, k):
        @pl.when(p - k >= 0)
        def _():
            o = f - 2 * k
            hop(g, row(g, o), o, 0, k, f).wait_recv()

            @pl.when(p < nl - 1)
            def _():
                hop(g, row(g, o), o, 0, k, f + 2).start()

            hop(g, row(g, o), o, 2, k, partner).start()

        @pl.when(p + k < nl)
        def _():
            o = f + 2 * k
            hop(g, row(g, o), o, 1, k, f).wait_recv()

            @pl.when(p > 0)
            def _():
                hop(g, row(g, o), o, 1, k, f - 2).start()

            hop(g, row(g, o), o, 3, k, partner).start()

    def arrive(g):
        pltpu.make_async_copy(ins[g], row(g, f), ls.at[g]).wait()
        for q in range(nl):
            o = q * 2 + 1 - c
            hop(g, row(g, o), o, 2, 0, partner).wait_recv()

    def sent(g):
        hop(g, ins[g], f, 2, 0, partner).wait_send()

        @pl.when(p < nl - 1)
        def _():
            hop(g, ins[g], f, 0, 0, f + 2).wait_send()

        @pl.when(p > 0)
        def _():
            hop(g, ins[g], f, 1, 0, f - 2).wait_send()

        for k in range(1, nl):
            @pl.when(p - k >= 0)
            def _():
                o = f - 2 * k

                @pl.when(p < nl - 1)
                def _():
                    hop(g, row(g, o), o, 0, k, f + 2).wait_send()

                hop(g, row(g, o), o, 2, k, partner).wait_send()

            @pl.when(p + k < nl)
            def _():
                o = f + 2 * k

                @pl.when(p > 0)
                def _():
                    hop(g, row(g, o), o, 1, k, f - 2).wait_send()

                hop(g, row(g, o), o, 3, k, partner).wait_send()

    def small_copy(k):
        return rcopy(small, small_s.at[f], ms.at[k], mr.at[k], {"fsdp": lax.rem(f + k, nf)})

    mine = pl.ds(s * rows, rows)
    own_small = pltpu.make_async_copy(small, small_s.at[f], ls.at[4])
    own_tok = pltpu.make_async_copy(tok, x_s.at[mine], ls.at[5])
    own_cot = pltpu.make_async_copy(cot, cot_s.at[mine], ls.at[6])

    for k in range(1, nf):
        small_copy(k).start()
    own_small.start()
    own_tok.start()
    seq_gather_start((tok,), (x_s,), xs, xr, px, py, s)
    own_send(0)
    own_send(1)
    own_cot.start()
    seq_gather_relay(0, tok, x_s, xs, xr, px, py, s)

    def cot_first():
        own = cot_s.at[mine]
        rcopy(cot, own, xs.at[1, 0], xr.at[1, 0], {"seq": px}).start()
        rcopy(cot, own, xs.at[1, 1], xr.at[1, 1], {"seq": py}).start()

    cot_first()
    step(0, 1)
    step(1, 1)
    own_send(2)

    own_small.wait()
    for k in range(1, nf):
        small_copy(k).wait()
    conv_s[...] = jnp.zeros_like(conv_s)
    pre_s[...] = jnp.zeros_like(pre_s)
    post_s[...] = jnp.zeros_like(post_s)
    heads = [jnp.zeros((8, 128), F32) for _ in range(3)]
    for i in range(nf):
        block = small_s[i]
        at, lanes, moved = place(block, i * (XBC // nf), XBC // nf)
        conv_s[:, at : at + lanes] += moved
        at, lanes, moved = place(block, i * (D // nf), D // nf)
        pre_s[:, at : at + lanes] += jnp.where(lax.broadcasted_iota(jnp.int32, moved.shape, 0) == 5, moved, 0.0)
        at, lanes, moved = place(block, i * (INNER // nf), INNER // nf)
        post_s[:, at : at + lanes] += jnp.where(lax.broadcasted_iota(jnp.int32, moved.shape, 0) == 6, moved, 0.0)
        for j in range(3):
            piece = block[:, 128 * j : 128 * j + 128]
            at = i * (HEADS // nf)
            heads[j] = heads[j] + (pltpu.roll(piece, at, 1) if at else piece)
    kw_s[:, 0:W] = conv_s[:, pl.ds(pl.multiple_of(s * W, 128), W)]
    kw_s[:, W:CH] = conv_s[:, INNER:XBC]
    lane1 = lax.broadcasted_iota(jnp.int32, (1, 128), 1)
    low1 = lane1 < HW
    back = lax.rem(128 - s * HL, 128)
    step_b, decay, skip = [pltpu.roll(h, back, 1)[7:8, :] for h in heads]
    hp_s[...] = jnp.zeros_like(hp_s)
    hp_s[0:1, :] = jnp.where(lane1 < HL, step_b, 0.0)
    hp_s[1:2, :] = jnp.where(lane1 < HL, -jnp.exp(decay), 0.0)
    ex_s[...] = jnp.zeros_like(ex_s)
    for i in range(HL // 2):
        ex_s[0:1, 128 * i : 128 * i + 128] = jnp.where(low1, spread(skip, 2 * i), spread(skip, 2 * i + 1))
    ex_s[1:2, :] = post_s[6:7, pl.ds(pl.multiple_of(s * W, 128), W)]

    for k in range(2, nl):
        step(0, k)
        step(1, k)
    own_tok.wait()
    seq_gather_finish(0, tok, x_s, xs, xr, px, py, s)
    seq_gather_relay(1, cot, cot_s, xs, xr, px, py, s)

    def norm(i, carry):
        r = pl.ds(pl.multiple_of(i * 128, 128), 128)
        x = x_s[r, :].astype(F32)
        rho = lax.rsqrt(jnp.sum(x * x, axis=1, keepdims=True) * (1.0 / D) + EPS)
        nrm_s[r, :] = (x * rho * pre_s[5:6, :]).astype(BF16)
        return carry

    lax.fori_loop(0, length // 128, norm, 0)
    step(2, 1)
    own_send(3)
    arrive(0)
    arrive(1)

    saves = [
        pltpu.make_async_copy(a, b, os_.at[i])
        for i, (a, b) in enumerate(
            (
                (x_s, x_out), (cot_s, cot_out), (nrm_s, nrm_out), (wv_s, wv_out), (ws_s, ws_out), (wg_s, wg_out),
                (wo_s, wo_out), (mix_s, mix_out), (gate_s, gate_out), (mixed_s, mixed_out), (st_s, st_out),
                (dsh_s, dsh_out),
            )
        )
    ]
    for i in (0, 2, 3, 4):
        saves[i].start()

    def project(i, carry):
        r = pl.ds(pl.multiple_of(i * 256, 256), 256)
        a = nrm_s[r, :]
        mix_s[r, 0:W] = nn(a, wv_s[...]).astype(BF16)
        mix_s[r, W:VC] = nn(a, ws_s[...]).astype(BF16)
        return carry

    lax.fori_loop(0, length // 256, project, 0)
    saves[7].start()

    def between(b):
        @pl.when(b == 0)
        def _():
            step(2, 2)

        @pl.when(b == 3)
        def _():
            for k in range(3, nl):
                step(2, k)

        @pl.when(b == 6)
        def _():
            step(3, 1)

    scan_fwd_blocks(
        mix_s.at[:, 0:W], mix_s.at[:, W:CH], mix_s.at[:, CH:VC], kw_s, hp_s, ex_s, mixed_s, st_s,
        buf, hst, xw_s, er_s, between,
    )
    for i in (9, 10):
        saves[i].start()
    arrive(2)
    saves[5].start()

    def project_gate(i, carry):
        r = pl.ds(pl.multiple_of(i * 256, 256), 256)
        gate_s[r, :] = nn(nrm_s[r, :], wg_s[...]).astype(BF16)
        return carry

    step(3, 2)
    lax.fori_loop(0, length // 256, project_gate, 0)
    saves[8].start()
    for k in range(3, nl):
        step(3, k)
    own_cot.wait()
    seq_gather_finish(1, cot, cot_s, xs, xr, px, py, s)
    saves[1].start()
    arrive(3)
    saves[6].start()
    eye = lax.broadcasted_iota(jnp.int32, (128, 128), 0) == lax.broadcasted_iota(jnp.int32, (128, 128), 1)

    def stats(i, carry):
        r = pl.ds(pl.multiple_of(i * 128, 128), 128)
        dsh = nn(cot_s[r, :], wo_s[...])
        dsh_s[r, :] = dsh
        gate = gate_s[r, :].astype(F32)
        gated = mixed_s[r, :].astype(F32) * (gate * sigmoid(gate))
        one = jnp.sum(gated * gated, axis=1, keepdims=True)
        two = jnp.sum(dsh * ex_s[1:2, :] * gated, axis=1, keepdims=True)
        stat_own[pl.ds(i, 1), :] = jnp.sum(jnp.where(eye, one, 0.0), axis=0, keepdims=True)
        stat_own[pl.ds(length // 128 + i, 1), :] = jnp.sum(jnp.where(eye, two, 0.0), axis=0, keepdims=True)
        return carry

    lax.fori_loop(0, length // 128, stats, 0)
    saves[11].start()
    copies = [rcopy(stat_own, stat_got.at[k], es.at[k], er.at[k], {"seq": s ^ k}) for k in range(1, SEQ)]
    for copy in copies:
        copy.start()
    for copy in copies:
        copy.wait()
    stat_s[...] = stat_own[...] + stat_got[1] + (stat_got[2] + stat_got[3])
    for g in range(GROUPS):
        sent(g)
    for save in saves:
        save.wait()


def front(nf, tok, cot, win, wst, wout, small):
    shape = jax.ShapeDtypeStruct
    dma = pltpu.SemaphoreType.DMA
    length = SEQ * tok.shape[0]
    big = [
        shape((length, D), BF16),
        shape((length, D), BF16),
        shape((length, D), BF16),
        shape((D, W), BF16),
        shape((D, VC - W), BF16),
        shape((D, W), BF16),
        shape((D, W), BF16),
        shape((length, VC), BF16),
        shape((length, W), BF16),
        shape((length, W), BF16),
        shape((length // Q, STATE, W), BF16),
        shape((length, W), F32),
    ]
    par = [
        shape((8, CH), F32),
        shape((8, 128), F32),
        shape((8, W), F32),
        shape((8, D), F32),
        shape((2 * length // 128, 128), F32),
    ]
    return pl.pallas_call(
        functools.partial(front_kernel, nf),
        out_shape=big + par,
        in_specs=[ANY] * 5 + [VMEM],
        out_specs=[ANY] * len(big) + [VMEM] * len(par),
        scratch_shapes=[pltpu.VMEM(b.shape, b.dtype) for b in big]
        + [
            pltpu.VMEM((nf, 8, 512), F32),
            pltpu.VMEM((8, XBC), F32),
            pltpu.VMEM((8, INNER), F32),
            pltpu.VMEM((2 * length // 128, 128), F32),
            pltpu.VMEM((SEQ, 2 * length // 128, 128), F32),
            pltpu.VMEM((Q + 8, CH), F32),
            pltpu.VMEM((STATE, W), F32),
            pltpu.VMEM((Q, W), BF16),
            pltpu.VMEM((8, W), F32),
            dma((2, 4)),
            dma((2, 4)),
            dma((GROUPS, 4, nf // 2)),
            dma((GROUPS, nf)),
            dma((nf,)),
            dma((nf,)),
            dma((SEQ,)),
            dma((SEQ,)),
            dma((7,)),
            dma((len(big),)),
        ],
        name="front",
        compiler_params=pltpu.CompilerParams(
            collective_id=1, has_side_effects=True, vmem_limit_bytes=VMEM_LIMIT
        ),
    )(tok, cot, win, wst, wout, small)


TN = (((0,), (0,)), ((), ()))
STRIP = 384


def unplace(block, at, width):
    start, shift = at // 128 * 128, at % 128
    lanes = -(-(width + shift) // 128) * 128
    piece = block[:, start : start + lanes]
    if shift:
        piece = pltpu.roll(piece, lanes - shift, 1)
    if lanes < 512:
        piece = jnp.concatenate([piece, jnp.zeros((piece.shape[0], 512 - lanes), piece.dtype)], axis=1)
    else:
        piece = piece[:, :512]
    return jnp.where(lax.broadcasted_iota(jnp.int32, piece.shape, 1) < width, piece, 0.0)


def back_kernel(
    nf, x_in, cot_in, nrm_in, wv_in, ws_in, wg_in, wo_in, mix_in, gate_in, mixed_in, st_in, dsh_in,
    kw_s, hp_s, ex_s, pre_s, stat_s,
    out_ref, gt_ref, go_ref, gg_ref, gv_ref, gs_ref, small_ref,
    xc_s, nrm_s, wv_s, ws_s, wg_s, wo_s, mix_s, gate_s, mixed_s, st_s, dsh_s,
    dy_s, dv_s, cotrow_s, part_s, ga_s, gb_s, gc_s,
    pb0, pb1, pb2, pb3, lb0, lb1, lb2, lb3, own0, own1, own2, own3,
    ab0, ab1, az0, az1,
    gcw_s, gch_s, ghd_s, gpost_s, gpre_s, conv_s, post_s, snd_s, got_s, sown_s, sgot_s,
    buf, cbuf, dhst, rowp, xw_s, e_s, er_s,
    ls, zs, zr, xs, xr, as_, ar, ms, mr, es, er, os_,
):
    s = lax.axis_index("seq")
    f = lax.axis_index("fsdp")
    px, py = s ^ 1, s ^ 2
    nl = nf // 2
    p, c = f // 2, f % 2
    partner = p * 2 + 1 - c
    bar = pltpu.get_barrier_semaphore()
    for k in range(1, SEQ):
        signal(bar, {"seq": s ^ k})
    for k in range(1, nf):
        signal(bar, {"fsdp": lax.rem(f + k, nf)})

    length = nrm_s.shape[0]
    rows = length // SEQ
    n = D // nf
    mine = pl.ds(s * rows, rows)
    loads = [
        pltpu.make_async_copy(a, b, ls.at[i])
        for i, (a, b) in enumerate(
            (
                (gate_in, gate_s), (mixed_in, mixed_s), (dsh_in, dsh_s), (cot_in, xc_s), (wo_in, wo_s),
                (nrm_in, nrm_s), (mix_in, mix_s), (st_in, st_s), (wg_in, wg_s), (wv_in, wv_s), (ws_in, ws_s),
                (cot_in.at[mine], cotrow_s), (x_in, xc_s),
            )
        )
    ]
    for load in loads[:-1]:
        load.start()
    pl.semaphore_wait(bar, nf - 1 + SEQ - 1)

    half = D // 2
    cols = (slice(0, half), slice(half, D))
    first, second = (px, py), (py, px)
    ab, az = (ab0, ab1), (az0, az1)

    def chunk(i, a):
        return part_s.at[pl.ds(i * rows, rows), cols[a]]

    def seq_one(t, a, m):
        i = (first[a] ^ second[a] ^ s) if m == 0 else first[a]
        return rcopy(chunk(i, a), ab[t].at[a, m], xs.at[t, a, m], xr.at[t, a, m], {"seq": first[a]})

    def seq_two(t, a):
        return rcopy(az[t].at[a, 0], az[t].at[a, 1], xs.at[t, a, 2], xr.at[t, a, 2], {"seq": second[a]})

    def add(*terms):
        total = terms[0].astype(F32)
        for term in terms[1:]:
            total = total + term.astype(F32)
        return total

    def seq_pass(t):
        for a in range(2):
            seq_one(t, a, 0).wait_recv()
            az[t][a, 0] = add(chunk(second[a], a)[...], ab[t][a, 0]).astype(BF16)
            seq_two(t, a).start()

    def seq_last(t, out):
        for a in range(2):
            seq_one(t, a, 1).wait_recv()
            seq_two(t, a).wait_recv()
            out[:, cols[a]] = add(chunk(s, a)[...], ab[t][a, 1], az[t][a, 1])

    def seq_sent(t):
        for a in range(2):
            seq_one(t, a, 0).wait_send()
            seq_one(t, a, 1).wait_send()
            seq_two(t, a).wait_send()

    parts = (ga_s, gb_s, ga_s, gc_s)
    pbs, lbs, owns = (pb0, pb1, pb2, pb3), (lb0, lb1, lb2, lb3), (own0, own1, own2, own3)
    gouts = (go_ref, gg_ref, gv_ref, gs_ref)

    def piece(g, i):
        return parts[g].at[pl.ds(pl.multiple_of(i * n, 16), n)]

    def swap(g, q):
        return rcopy(piece(g, q * 2 + 1 - c), pbs[g].at[q], zs.at[g, 0, q], zr.at[g, 0, q], {"fsdp": partner})

    def up(g, q):
        return rcopy(pbs[g].at[q], lbs[g].at[q], zs.at[g, 1, q], zr.at[g, 1, q], {"fsdp": f + 2})

    def down(g, q):
        to = jnp.where(q == p - 1, nl, q)
        return rcopy(pbs[g].at[q], lbs[g].at[to], zs.at[g, 2, q], zr.at[g, 2, q], {"fsdp": f - 2})

    def slot(g, t):
        @pl.when(p <= t)
        def _():
            q = nl - 1 - t + p
            swap(g, q).wait_recv()

            @pl.when(p > 0)
            def _():
                up(g, q).wait_recv()
                pbs[g][q] = add(piece(g, q * 2 + c)[...], pbs[g][q], lbs[g][q]).astype(BF16)

            @pl.when(p == 0)
            def _():
                pbs[g][q] = add(piece(g, q * 2 + c)[...], pbs[g][q]).astype(BF16)

            up(g, q).start()

        @pl.when(nl - 1 - p <= t)
        def _():
            q = t - (nl - 1 - p)
            swap(g, q).wait_recv()

            @pl.when(p < nl - 1)
            def _():
                down(g, q).wait_recv()
                pbs[g][q] = add(piece(g, q * 2 + c)[...], pbs[g][q], lbs[g][q]).astype(BF16)

            @pl.when(p == nl - 1)
            def _():
                pbs[g][q] = add(piece(g, q * 2 + c)[...], pbs[g][q]).astype(BF16)

            down(g, q).start()

    def close(g):
        swap(g, p).wait_recv()

        @pl.when(p > 0)
        def _():
            up(g, p).wait_recv()

        @pl.when(p < nl - 1)
        def _():
            down(g, p).wait_recv()

        @pl.when(p == 0)
        def _():
            owns[g][...] = add(piece(g, f)[...], pbs[g][p], lbs[g][nl]).astype(BF16)

        @pl.when(p == nl - 1)
        def _():
            owns[g][...] = add(piece(g, f)[...], pbs[g][p], lbs[g][p]).astype(BF16)

        @pl.when(jnp.logical_and(p > 0, p < nl - 1))
        def _():
            owns[g][...] = add(piece(g, f)[...], pbs[g][p], lbs[g][p], lbs[g][nl]).astype(BF16)

        place_ = gouts[g].at[pl.ds(s * n, n)]
        rcopy(owns[g], place_, as_.at[g, 0], ar.at[g, 0], {"seq": px}).start()
        rcopy(owns[g], place_, as_.at[g, 1], ar.at[g, 1], {"seq": py}).start()
        pltpu.make_async_copy(owns[g], place_, os_.at[g]).start()

    def relay(g):
        seq_gather_relay(g, owns[g], gouts[g], as_, ar, px, py, s)

    def swaps_sent(g):
        for q in range(nl):
            swap(g, q).wait_send()

    def line_sent(g):
        for q in range(nl):
            @pl.when(q > p)
            def _():
                up(g, q).wait_send()

            @pl.when(q < p)
            def _():
                down(g, q).wait_send()

    order = []
    for k in range(D // STRIP // 2):
        order += [D // STRIP - 1 - k, k]

    def strip(j, a_ref, b_ref, bcols, g):
        at = slice(j * STRIP, (j + 1) * STRIP)
        parts[g][at, :] = lax.dot_general(a_ref[:, at], b_ref[:, bcols], TN, preferred_element_type=F32).astype(BF16)
        for q in range(nl):
            if j * STRIP <= q * 2 * n < (j + 1) * STRIP:
                swap(g, q).start()

    for i in range(3):
        loads[i].wait()
    eye = lax.broadcasted_iota(jnp.int32, (128, 128), 0) == lax.broadcasted_iota(jnp.int32, (128, 128), 1)
    gpost_s[...] = jnp.zeros_like(gpost_s)

    def gated_norm(i, carry):
        r = pl.ds(pl.multiple_of(i * 128, 128), 128)
        one = jnp.sum(jnp.where(eye, stat_s[pl.ds(i, 1), :], 0.0), axis=1, keepdims=True)
        two = jnp.sum(jnp.where(eye, stat_s[pl.ds(length // 128 + i, 1), :], 0.0), axis=1, keepdims=True)
        rho = lax.rsqrt(one * (1.0 / INNER) + EPS)
        mean = rho * two * (1.0 / INNER)
        gate = gate_s[r, :].astype(F32)
        mixed = mixed_s[r, :].astype(F32)
        dsh = dsh_s[r, :]
        post = ex_s[1:2, :]
        sg = sigmoid(gate)
        sl = gate * sg
        n1 = mixed * sl * rho
        gpost_s[0:1, :] += jnp.sum(dsh * n1, axis=0, keepdims=True)
        d_gated = rho * (dsh * post - n1 * mean)
        mixed_s[r, :] = (n1 * post).astype(BF16)
        dy_s[r, :] = (d_gated * sl).astype(BF16)
        gate_s[r, :] = (d_gated * mixed * (sg * (1.0 + gate * (1.0 - sg)))).astype(BF16)
        return carry

    lax.fori_loop(0, length // 128, gated_norm, 0)

    every = slice(0, W)
    loads[3].wait()
    for j in order:
        strip(j, xc_s, mixed_s, every, 0)
    loads[-1].start()
    slot(0, 0)

    loads[4].wait()

    def out_part(i, carry):
        r = pl.ds(pl.multiple_of(i * rows, rows), rows)
        part_s[r, :] = nt(mixed_s[r, :], wo_s[...]).astype(BF16)
        return carry

    lax.fori_loop(0, SEQ, out_part, 0)
    for m in range(2):
        for a in range(2):
            seq_one(0, a, m).start()

    loads[5].wait()
    for j in order:
        strip(j, nrm_s, gate_s, every, 1)
    slot(0, 1)
    slot(1, 0)
    loads[6].wait()
    loads[7].wait()

    def between(i):
        @pl.when(i == 1)
        def _():
            for t in range(2, nl - 1):
                slot(0, t)

        @pl.when(i == 2)
        def _():
            seq_pass(0)

        @pl.when(i == 3)
        def _():
            close(0)
            slot(1, 1)

        @pl.when(i == 5)
        def _():
            for t in range(2, nl - 1):
                slot(1, t)
            relay(0)

    scan_bwd_blocks(
        mix_s.at[:, 0:W], mix_s.at[:, W:CH], mix_s.at[:, CH:VC], dy_s, st_s, kw_s, hp_s, ex_s,
        dv_s, gcw_s, gch_s, ghd_s, buf, cbuf, dhst, rowp, xw_s, e_s, er_s, between,
    )

    loads[-1].wait()
    out_ref[...] = xc_s[mine, :].astype(F32)
    for a in range(2):
        seq_one(0, a, 1).wait_recv()
        seq_two(0, a).wait_recv()
        out_ref[:, cols[a]] += add(chunk(s, a)[...], ab0[a, 1], az0[a, 1])
    seq_sent(0)
    close(1)
    swaps_sent(0)
    for i, j in enumerate(order):
        strip(j, nrm_s, dv_s, every, 2)
        strip(j, nrm_s, dv_s, slice(W, VC), 3)
        if i == 1:
            slot(2, 0)
            slot(3, 0)
    relay(1)

    for i in range(8, 12):
        loads[i].wait()
    gpre_s[...] = jnp.zeros_like(gpre_s)

    def dn_part(i, carry):
        r = pl.ds(pl.multiple_of((s ^ (SEQ - 1 - i)) * rows, rows), rows)
        dn = nt(gate_s[r, :], wg_s[...]) + nt(dv_s[r, 0:W], wv_s[...]) + nt(dv_s[r, W:VC], ws_s[...])
        part_s[r, :] = dn.astype(BF16)
        x = xc_s[r, :].astype(F32)
        rho = lax.rsqrt(jnp.sum(x * x, axis=1, keepdims=True) * (1.0 / D) + EPS)
        gpre_s[5:6, :] += jnp.sum(dn * (x * rho), axis=0, keepdims=True)

        @pl.when(i == 0)
        def _():
            for a in range(2):
                seq_one(1, a, 0).start()

        @pl.when(i == 2)
        def _():
            for a in range(2):
                seq_one(1, a, 1).start()
            for g in (2, 3):
                for t in range(1, min(2, nl - 1)):
                    slot(g, t)

        return carry

    lax.fori_loop(0, SEQ, dn_part, 0)

    conv_s[...] = jnp.zeros_like(conv_s)
    conv_s[:, pl.ds(pl.multiple_of(s * W, 128), W)] = gcw_s[:, 0:W]
    conv_s[:, INNER:XBC] = gcw_s[:, W:CH]
    post_s[...] = jnp.zeros_like(post_s)
    post_s[6:7, pl.ds(pl.multiple_of(s * W, 128), W)] = gpost_s[0:1, :]
    lane8 = lax.broadcasted_iota(jnp.int32, (8, 128), 1)
    row8 = lax.broadcasted_iota(jnp.int32, (8, 128), 0)
    skip = jnp.zeros((1, 128), F32)
    lane1 = lax.broadcasted_iota(jnp.int32, (1, 128), 1)
    for h in range(HL):
        at = slice(128 * (h // 2), 128 * (h // 2) + 128)
        half_of = (lane1 < HW) if h % 2 == 0 else (lane1 >= HW)
        skip = jnp.where(lane1 == h, jnp.sum(jnp.where(half_of, gch_s[0:1, at], 0.0), axis=1, keepdims=True), skip)
    heads = [
        pltpu.roll(jnp.where(row8 == 7, jnp.broadcast_to(v, (8, 128)), 0.0), s * HL, 1)
        for v in (ghd_s[0:1, :], ghd_s[1:2, :], skip)
    ]
    row512 = lax.broadcasted_iota(jnp.int32, (8, 512), 0)
    hn = HEADS // nf
    for i in range(nf):
        conv = unplace(conv_s, i * (XBC // nf), XBC // nf)
        block = jnp.where(row512 < 5, conv, 0.0)
        block = block + unplace(gpre_s, i * (D // nf), D // nf)
        block = block + unplace(post_s, i * (INNER // nf), INNER // nf)
        tiles = []
        for v in heads:
            moved = pltpu.roll(v, (128 - i * hn) % 128, 1) if i else v
            tiles.append(jnp.where(lane8 < hn, moved, 0.0))
        block = block + jnp.concatenate(tiles + [jnp.zeros((8, 128), F32)], axis=1)
        snd_s[i] = block

    def small_send(k):
        to = lax.rem(f + k, nf)
        return rcopy(snd_s.at[to], got_s.at[k], ms.at[k], mr.at[k], {"fsdp": to})

    for k in range(1, nf):
        small_send(k).start()
    seq_pass(1)
    for g in (2, 3):
        for t in range(2, nl - 1):
            slot(g, t)
    total = snd_s[f]
    for k in range(1, nf):
        small_send(k).wait_recv()
        total = total + got_s[k]
    sown_s[...] = total

    def small_share(k):
        return rcopy(sown_s, sgot_s.at[s], es.at[k], er.at[k], {"seq": s ^ k})

    for k in range(1, SEQ):
        small_share(k).start()
    close(2)
    close(3)
    relay(2)
    relay(3)

    for a in range(2):
        seq_one(1, a, 1).wait_recv()
        seq_two(1, a).wait_recv()
        gt_ref[:, cols[a]] = add(chunk(s, a)[...], ab1[a, 1], az1[a, 1])

    def grad_tokens(i, carry):
        r = pl.ds(pl.multiple_of(i * 64, 64), 64)
        x = xc_s[pl.ds(pl.multiple_of(s * rows + i * 64, 64), 64), :].astype(F32)
        rho = lax.rsqrt(jnp.sum(x * x, axis=1, keepdims=True) * (1.0 / D) + EPS)
        n0 = x * rho
        e0 = gt_ref[r, :] * pre_s[5:6, :]
        mean = jnp.sum(e0 * n0, axis=1, keepdims=True) * (1.0 / D)
        gt_ref[r, :] = cotrow_s[r, :].astype(F32) + rho * (e0 - n0 * mean)
        return carry

    lax.fori_loop(0, rows // 64, grad_tokens, 0)

    for k in range(1, SEQ):
        small_share(k).wait()
    total = jnp.zeros_like(sown_s)
    for k in range(SEQ):
        total = total + jnp.where(s == k, sown_s[...], sgot_s[k])
    small_ref[...] = total
    for k in range(1, nf):
        small_send(k).wait_send()
    seq_sent(1)
    for g in range(4):
        seq_gather_finish(g, owns[g], gouts[g], as_, ar, px, py, s)
        pltpu.make_async_copy(owns[g], gouts[g].at[pl.ds(s * n, n)], os_.at[g]).wait()
        line_sent(g)
    for g in range(1, 4):
        swaps_sent(g)


def back(nf, big, par):
    shape = jax.ShapeDtypeStruct
    vm = pltpu.VMEM
    dma = pltpu.SemaphoreType.DMA
    length = big[0].shape[0]
    rows = length // SEQ
    nl = nf // 2
    n = D // nf
    widths = (W, W, W, VC - W)
    boxes = [vm((nl, n, w), BF16) for w in widths] + [vm((nl + 1, n, w), BF16) for w in widths]
    boxes += [vm((n, w), BF16) for w in widths]
    return pl.pallas_call(
        functools.partial(back_kernel, nf),
        out_shape=[shape((rows, D), F32)] * 2 + [shape((SEQ * n, w), BF16) for w in widths] + [shape((8, 512), F32)],
        in_specs=[ANY] * len(big) + [VMEM] * len(par),
        out_specs=[VMEM] * 2 + [ANY] * 4 + [VMEM],
        scratch_shapes=[
            vm((length, D), BF16),
            vm((length, D), BF16),
            vm((D, W), BF16),
            vm((D, VC - W), BF16),
            vm((D, W), BF16),
            vm((D, W), BF16),
            vm((length, VC), BF16),
            vm((length, W), BF16),
            vm((length, W), BF16),
            vm((length // Q, STATE, W), BF16),
            vm((length, W), F32),
            vm((length, W), BF16),
            vm((length, VC), BF16),
            vm((rows, D), BF16),
            vm((length, D), BF16),
            vm((D, W), BF16),
            vm((D, W), BF16),
            vm((D, VC - W), BF16),
        ]
        + boxes
        + [vm((2, 2, rows, D // 2), BF16)] * 4
        + [
            vm((8, CH), F32),
            vm((8, W), F32),
            vm((8, 128), F32),
            vm((8, W), F32),
            vm((8, D), F32),
            vm((8, XBC), F32),
            vm((8, INNER), F32),
            vm((nf, 8, 512), F32),
            vm((nf, 8, 512), F32),
            vm((8, 512), F32),
            vm((SEQ, 8, 512), F32),
            vm((Q + 8, CH), F32),
            vm((Q + 8, CH), F32),
            vm((STATE, W), F32),
            vm((128, Q), F32),
            vm((Q, W), BF16),
            vm((Q, W), BF16),
            vm((8, W), F32),
            dma((13,)),
            dma((4, 3, nl)),
            dma((4, 3, nl)),
            dma((2, 2, 3)),
            dma((2, 2, 3)),
            dma((4, 4)),
            dma((4, 4)),
            dma((nf,)),
            dma((nf,)),
            dma((SEQ,)),
            dma((SEQ,)),
            dma((4,)),
        ],
        name="back",
        compiler_params=pltpu.CompilerParams(
            collective_id=2, has_side_effects=True, vmem_limit_bytes=67043328
        ),
    )(*big, *par)


def own_rows(array, index, row_count):
    return lax.dynamic_slice_in_dim(array, index * row_count, row_count, 0)


def body(
    tokens,
    input_projection_weight,
    pre_gain,
    conv_weight,
    conv_bias,
    step_bias,
    decay_log,
    skip_gain,
    post_gain,
    output_projection_weight,
    cotangent,
):
    nf = lax.axis_size("fsdp")
    s = lax.axis_index("seq")
    tok = tokens.reshape(tokens.shape[1:])
    cot = cotangent.reshape(cotangent.shape[1:])
    win = input_projection_weight
    n = win.shape[0]

    w_state = jnp.concatenate(
        [
            win[:, 2 * INNER : 2 * INNER + 2 * STATE],
            lax.dynamic_slice(win, (0, 2 * INNER + 2 * STATE + s * HL), (n, HL)),
            jnp.zeros((n, 128 - HL), BF16),
        ],
        axis=1,
    )
    w_out = own_rows(output_projection_weight, s, W).T

    def line(*pieces):
        return jnp.concatenate([jnp.pad(v[None], ((0, 0), (0, 128 * t - v.shape[0]))) for v, t in pieces], axis=1)

    small = jnp.concatenate(
        [
            jnp.pad(conv_weight.T, ((0, 0), (0, 512 - conv_weight.shape[0]))),
            line((conv_bias, 4)),
            line((pre_gain, 4)),
            line((post_gain, 4)),
            line((step_bias, 1), (decay_log, 1), (skip_gain, 2)),
        ]
    ).astype(F32)
    outs = front(nf, tok, cot, win, w_state, w_out, small)
    block_out, grad_tokens, g_out, g_gate, g_val, g_state, small = back(nf, outs[:12], outs[12:])

    g_gate = g_gate.reshape(SEQ, n, W).astype(F32)
    g_val = g_val.reshape(SEQ, n, W).astype(F32)
    g_state = g_state.reshape(SEQ, n, VC - W).astype(F32)
    grad_in = jnp.concatenate(
        [g_gate[i] for i in range(SEQ)]
        + [g_val[i] for i in range(SEQ)]
        + [jnp.sum(g_state[:, :, : 2 * STATE], axis=0)]
        + [g_state[i, :, 2 * STATE : 2 * STATE + HL] for i in range(SEQ)],
        axis=1,
    )
    grad_out = jnp.swapaxes(g_out.reshape(SEQ, n, W), 1, 2).reshape(INNER, n).astype(F32)
    nc = XBC // nf
    nh = HEADS // nf
    grad_cw, grad_cb = small[:4, :nc].T, small[4, :nc]
    grad_pre, grad_post = small[5, :n], small[6, : INNER // nf]
    grad_step, grad_decay, grad_skip = [small[7, 128 * i : 128 * i + nh] for i in range(3)]
    return (
        block_out[None],
        grad_tokens[None],
        grad_in,
        grad_pre,
        grad_cw,
        grad_cb,
        grad_step,
        grad_decay,
        grad_skip,
        grad_post,
        grad_out,
    )


def solution(mesh):
    in_specs = (
        P("fsdp", "seq", None),
        P("fsdp", None),
        P("fsdp"),
        P("fsdp", None),
        P("fsdp"),
        P("fsdp"),
        P("fsdp"),
        P("fsdp"),
        P("fsdp"),
        P(None, "fsdp"),
        P("fsdp", "seq", None),
    )
    out_specs = (
        P("fsdp", "seq", None),
        P("fsdp", "seq", None),
        P("fsdp", None),
        P("fsdp"),
        P("fsdp", None),
        P("fsdp"),
        P("fsdp"),
        P("fsdp"),
        P("fsdp"),
        P("fsdp"),
        P(None, "fsdp"),
    )
    return jax.shard_map(body, mesh=mesh, in_specs=in_specs, out_specs=out_specs, check_vma=False)
```

profile of v0, /device:TPU:8, one launch (start us, length us, event | category | flops | bytes accessed | tf_op | source)
XLA Modules:
  0.0 237.7 jit_solution(14025168894724756288)
XLA Ops:
  1.4 0.7 broadcast_in_dim.30
  2.1 0.7 broadcast_in_dim.28
  2.8 0.7 fusion.1
  3.5 0.7 pad.27
  4.8 0.9 constant_dynamic-slice_fusion
  5.7 0.9 slice.71
  6.6 0.7 maximum_maximum_fusion.wst
  7.3 1.7 dynamic-slice_bitcast_fusion.wout
  9.0 88.6 %front.1 = (bf16[1024,1536]{1,0:T(8,128)(2,1)}, bf16[1024,1536]{1,0:T(8,128)(2,1)}, bf16[1024,1536]{1,0:T(8,128)(2,1)}, bf16[1536,768]{1,0:T(8,128)(2,1)}, bf16[...) custom-call(bf16[256,1536]{1,0:T(8,128)(2,1)} %bitcast.40, ...), custom_call_target="tpu_custom_call" | custom-call | tf_op jit(solution)/shard_map/front/pallas_call | solution.py:602
  97.6 117.5 %back.1 = (f32[256,1536]{1,0:T(8,128)}, f32[256,1536]{1,0:T(8,128)}, bf16[768,768]{1,0:T(8,128)(2,1)}, bf16[768,768]{1,0:T(8,128)(2,1)}, bf16[768,768]{1,0:T(8,1...) custom-call(bf16[1024,1536]{1,0:T(8,128)(2,1)} %get-tuple-element.35.x_in, ...), custom_call_target="tpu_custom_call" | custom-call | tf_op jit(solution)/shard_map/back/pallas_call | solution.py:1068
  215.2 1.3 slice.85
  216.4 1.2 slice_bitcast_fusion.5
  217.6 1.3 slice_reduce_fusion.1
  218.9 1.3 slice.87
  220.2 1.3 slice_bitcast_fusion.4
  221.5 1.2 convert.4
  222.8 0.7 slice_reduce_fusion
  223.5 0.8 slice_bitcast_fusion
  224.5 1.7 copy.23
  226.2 0.8 copy-done.1
  226.9 1.4 fusion.2
  228.4 5.3 %concatenate.15 = f32[192,6448]{1,0:T(8,128)} concatenate(f32[192,768]{1,0:T(8,128)S(1)} %get-tuple-element.74, f32[192,768]{1,0:T(8,128)S(1)} %get-tuple-element.75, f32[192,768]{1,0:T(8,128)} %get-tuple-element.76, f32[192,768]{1,0:T(8,128)} %get-tuple-element.77, f32[192,768]{1,0:T(8,128)S(1)} %get-tuple-element.66, f32[192,768]{1,0:T(8,128)S(1)} %get-tuple-element.65, ...), dimensions={1} | concatenate | bytes 9904128 | tf_op jit(solution)/shard_map/concatenate | solution.py:1186
  233.7 2.8 %copy.26 = f32[1,256,1536]{2,1,0:T(8,128)} copy(f32[1,256,1536]{2,1,0:T(8,128)} %bitcast.38) | data formatting | bytes 3145728
  236.5 1.1 copy.27
  (16 shorter events, 1.6 us)
Async XLA Ops:
  221.5 2.7 %copy-start.3 = (bf16[768,768]{1,0:T(8,128)(2,1)S(1)}, bf16[768,768]{1,0:T(8,128)(2,1)}, u32[]{:S(2)}) copy-start(bf16[768,768]{1,0:T(8,128)(2,1)} %get-tuple-element.58) | copy-start | bytes 3538948
  224.5 1.7 copy-start
  224.5 2.5 %copy-start.1 = (bf16[768,768]{1,0:T(8,128)(2,1)S(1)}, bf16[768,768]{1,0:T(8,128)(2,1)}, u32[]{:S(2)}) copy-start(bf16[768,768]{1,0:T(8,128)(2,1)} %get-tuple-element.55) | copy-start | bytes 3538948
  233.7 2.8 %copy-start.2 = (f32[256,1536]{1,0:T(8,128)S(1)}, f32[256,1536]{1,0:T(8,128)}, u32[]{:S(2)}) copy-start(f32[256,1536]{1,0:T(8,128)} %get-tuple-element.53) | copy-start | bytes 4718596
where the time goes:
time: 241 us; the launch traced here: 238 us
  Pallas kernels  206 us (85%)
  local copies, waits for them, and re-layouts  26.7 us (11%)
  other arithmetic  4.14 us (2%)
    pallas_call x1, Pallas kernels, back(): pl.pallas_call(functools.partial(back_kernel, nf), out_shape=[shape((rows...  118 us
    pallas_call x1, Pallas kernels, front(): pl.pallas_call(functools.partial(front_kernel, nf), out_shape=big + par,...  88.6 us
    concatenate x1, local copies, waits for them, and re-layouts, body(): jnp.concatenate([g_gate[i] for i in range(SEQ)] + [g_val[i] for i in rang...  5.33 us

commit v1 on v0

--- a/solution.py
+++ b/solution.py
@@ -89,7 +89,8 @@
 
 
 def rates_of(r_ref, rows, hp_ref, tri):
-    raw = r_ref[rows, :].astype(F32) + hp_ref[0:1, :]
+    back = lax.rem(128 - lax.axis_index("seq") * HL, 128)
+    raw = pltpu.roll(r_ref[rows, :].astype(F32), back, 1) + hp_ref[0:1, :]
     dt = softplus(raw)
     lam = nn(tri, dt * hp_ref[1:2, :], HIGH)
     return raw, dt, lam
@@ -257,7 +258,7 @@
         d_rate = (col_n + col_i + hp_ref[1:2, :] * after) * sigmoid(raw)
         ghd_ref[0:1, :] += jnp.sum(d_rate, axis=0, keepdims=True)
         ghd_ref[1:2, :] += jnp.sum(dt * after, axis=0, keepdims=True) * hp_ref[1:2, :]
-        dv_ref[rows, CH:VC] = d_rate.astype(BF16)
+        dv_ref[rows, CH:VC] = pltpu.roll(d_rate, lax.axis_index("seq") * HL, 1).astype(BF16)
         for at in (slice(0, W), slice(W, CH)):
             raw_v = cbuf[8 : 8 + Q, at]
             dk = buf[0:Q, at]
@@ -321,7 +322,7 @@
         win.at[:, pl.ds(pl.multiple_of(INNER + s * W, 128), W)],
         wst,
         win.at[:, pl.ds(pl.multiple_of(s * W, 128), W)],
-        wout,
+        wout.at[:, pl.ds(pl.multiple_of(s * W, 128), W)],
     )
     outs = (wv_s, ws_s, wg_s, wo_s)
 
@@ -420,17 +421,12 @@
     own_send(0)
     own_send(1)
     own_cot.start()
-    seq_gather_relay(0, tok, x_s, xs, xr, px, py, s)
-
-    def cot_first():
-        own = cot_s.at[mine]
-        rcopy(cot, own, xs.at[1, 0], xr.at[1, 0], {"seq": px}).start()
-        rcopy(cot, own, xs.at[1, 1], xr.at[1, 1], {"seq": py}).start()
-
-    cot_first()
     step(0, 1)
     step(1, 1)
-    own_send(2)
+    seq_gather_relay(0, tok, x_s, xs, xr, px, py, s)
+    own = cot_s.at[mine]
+    rcopy(cot, own, xs.at[1, 0], xr.at[1, 0], {"seq": px}).start()
+    rcopy(cot, own, xs.at[1, 1], xr.at[1, 1], {"seq": py}).start()
 
     own_small.wait()
     for k in range(1, nf):
@@ -468,9 +464,14 @@
     for k in range(2, nl):
         step(0, k)
         step(1, k)
+        if k == 2:
+            own_send(2)
+            own_send(3)
+    if nl < 3:
+        own_send(2)
+        own_send(3)
     own_tok.wait()
     seq_gather_finish(0, tok, x_s, xs, xr, px, py, s)
-    seq_gather_relay(1, cot, cot_s, xs, xr, px, py, s)
 
     def norm(i, carry):
         r = pl.ds(pl.multiple_of(i * 128, 128), 128)
@@ -480,8 +481,6 @@
         return carry
 
     lax.fori_loop(0, length // 128, norm, 0)
-    step(2, 1)
-    own_send(3)
     arrive(0)
     arrive(1)
 
@@ -506,21 +505,21 @@
         return carry
 
     lax.fori_loop(0, length // 256, project, 0)
+    step(2, 1)
     saves[7].start()
 
     def between(b):
-        @pl.when(b == 0)
+        @pl.when(b == 1)
+        def _():
+            seq_gather_relay(1, cot, cot_s, xs, xr, px, py, s)
+
+        @pl.when(b == 2)
+        def _():
+            step(3, 1)
+
+        @pl.when(b == 5)
         def _():
             step(2, 2)
-
-        @pl.when(b == 3)
-        def _():
-            for k in range(3, nl):
-                step(2, k)
-
-        @pl.when(b == 6)
-        def _():
-            step(3, 1)
 
     scan_fwd_blocks(
         mix_s.at[:, 0:W], mix_s.at[:, W:CH], mix_s.at[:, CH:VC], kw_s, hp_s, ex_s, mixed_s, st_s,
@@ -528,6 +527,9 @@
     )
     for i in (9, 10):
         saves[i].start()
+    step(3, 2)
+    for k in range(3, nl):
+        step(2, k)
     arrive(2)
     saves[5].start()
 
@@ -536,7 +538,6 @@
         gate_s[r, :] = nn(nrm_s[r, :], wg_s[...]).astype(BF16)
         return carry
 
-    step(3, 2)
     lax.fori_loop(0, length // 256, project_gate, 0)
     saves[8].start()
     for k in range(3, nl):
@@ -725,11 +726,10 @@
             seq_two(t, a).wait_recv()
             out[:, cols[a]] = add(chunk(s, a)[...], ab[t][a, 1], az[t][a, 1])
 
-    def seq_sent(t):
+    def seq_one_sent(t):
         for a in range(2):
             seq_one(t, a, 0).wait_send()
             seq_one(t, a, 1).wait_send()
-            seq_two(t, a).wait_send()
 
     parts = (ga_s, gb_s, ga_s, gc_s)
     pbs, lbs, owns = (pb0, pb1, pb2, pb3), (lb0, lb1, lb2, lb3), (own0, own1, own2, own3)
@@ -748,38 +748,40 @@
         to = jnp.where(q == p - 1, nl, q)
         return rcopy(pbs[g].at[q], lbs[g].at[to], zs.at[g, 2, q], zr.at[g, 2, q], {"fsdp": f - 2})
 
+    def send_up(g, q, terms):
+        pbs[g][q] = add(piece(g, q * 2 + c)[...], pbs[g][q], *terms).astype(BF16)
+        up(g, q).start()
+
+    def send_down(g, q, terms):
+        pbs[g][q] = add(piece(g, q * 2 + c)[...], pbs[g][q], *terms).astype(BF16)
+        down(g, q).start()
+
+    def ends(g, shards):
+        for k in shards:
+            @pl.when(p == 0)
+            def _():
+                swap(g, nl - 1 - k).wait_recv()
+                send_up(g, nl - 1 - k, ())
+
+            @pl.when(p == nl - 1)
+            def _():
+                swap(g, k).wait_recv()
+                send_down(g, k, ())
+
     def slot(g, t):
-        @pl.when(p <= t)
+        @pl.when(jnp.logical_and(p > 0, p <= t))
         def _():
             q = nl - 1 - t + p
             swap(g, q).wait_recv()
-
-            @pl.when(p > 0)
-            def _():
-                up(g, q).wait_recv()
-                pbs[g][q] = add(piece(g, q * 2 + c)[...], pbs[g][q], lbs[g][q]).astype(BF16)
-
-            @pl.when(p == 0)
-            def _():
-                pbs[g][q] = add(piece(g, q * 2 + c)[...], pbs[g][q]).astype(BF16)
-
-            up(g, q).start()
-
-        @pl.when(nl - 1 - p <= t)
+            up(g, q).wait_recv()
+            send_up(g, q, (lbs[g][q],))
+
+        @pl.when(jnp.logical_and(p < nl - 1, nl - 1 - p <= t))
         def _():
             q = t - (nl - 1 - p)
             swap(g, q).wait_recv()
-
-            @pl.when(p < nl - 1)
-            def _():
-                down(g, q).wait_recv()
-                pbs[g][q] = add(piece(g, q * 2 + c)[...], pbs[g][q], lbs[g][q]).astype(BF16)
-
-            @pl.when(p == nl - 1)
-            def _():
-                pbs[g][q] = add(piece(g, q * 2 + c)[...], pbs[g][q]).astype(BF16)
-
-            down(g, q).start()
+            down(g, q).wait_recv()
+            send_down(g, q, (lbs[g][q],))
 
     def close(g):
         swap(g, p).wait_recv()
@@ -865,48 +867,61 @@
     lax.fori_loop(0, length // 128, gated_norm, 0)
 
     every = slice(0, W)
+    loads[4].wait()
+
+    def out_part(i, carry):
+        r = pl.ds(pl.multiple_of((s ^ (SEQ - 1 - i)) * rows, rows), rows)
+        part_s[r, :] = nt(mixed_s[r, :], wo_s[...]).astype(BF16)
+
+        @pl.when(i == 0)
+        def _():
+            for a in range(2):
+                seq_one(0, a, 0).start()
+
+        @pl.when(i == 2)
+        def _():
+            for a in range(2):
+                seq_one(0, a, 1).start()
+
+        return carry
+
+    lax.fori_loop(0, SEQ, out_part, 0)
     loads[3].wait()
     for j in order:
         strip(j, xc_s, mixed_s, every, 0)
     loads[-1].start()
-    slot(0, 0)
-
-    loads[4].wait()
-
-    def out_part(i, carry):
-        r = pl.ds(pl.multiple_of(i * rows, rows), rows)
-        part_s[r, :] = nt(mixed_s[r, :], wo_s[...]).astype(BF16)
-        return carry
-
-    lax.fori_loop(0, SEQ, out_part, 0)
-    for m in range(2):
-        for a in range(2):
-            seq_one(0, a, m).start()
+    ends(0, range(nl - 1))
 
     loads[5].wait()
     for j in order:
         strip(j, nrm_s, gate_s, every, 1)
-    slot(0, 1)
-    slot(1, 0)
+    ends(1, range(nl - 1))
     loads[6].wait()
     loads[7].wait()
 
     def between(i):
+        @pl.when(i == 0)
+        def _():
+            slot(0, 1)
+
         @pl.when(i == 1)
+        def _():
+            seq_pass(0)
+
+        @pl.when(i == 2)
         def _():
             for t in range(2, nl - 1):
                 slot(0, t)
 
-        @pl.when(i == 2)
-        def _():
-            seq_pass(0)
-
         @pl.when(i == 3)
         def _():
             close(0)
+
+        @pl.when(i == 4)
+        def _():
             slot(1, 1)
 
-        @pl.when(i == 5)
+        @pl.when(i == 6)
         def _():
             for t in range(2, nl - 1):
                 slot(1, t)
@@ -918,22 +933,8 @@
     )
 
     loads[-1].wait()
-    out_ref[...] = xc_s[mine, :].astype(F32)
-    for a in range(2):
-        seq_one(0, a, 1).wait_recv()
-        seq_two(0, a).wait_recv()
-        out_ref[:, cols[a]] += add(chunk(s, a)[...], ab0[a, 1], az0[a, 1])
-    seq_sent(0)
-    close(1)
     swaps_sent(0)
-    for i, j in enumerate(order):
-        strip(j, nrm_s, dv_s, every, 2)
-        strip(j, nrm_s, dv_s, slice(W, VC), 3)
-        if i == 1:
-            slot(2, 0)
-            slot(3, 0)
-    relay(1)
-
+    seq_one_sent(0)
     for i in range(8, 12):
         loads[i].wait()
     gpre_s[...] = jnp.zeros_like(gpre_s)
@@ -950,17 +951,39 @@
         def _():
             for a in range(2):
                 seq_one(1, a, 0).start()
+            for j in order[2:]:
+                strip(j, nrm_s, dv_s, every, 2)
+            ends(2, range(1, nl - 1))
 
         @pl.when(i == 2)
         def _():
             for a in range(2):
                 seq_one(1, a, 1).start()
-            for g in (2, 3):
-                for t in range(1, min(2, nl - 1)):
-                    slot(g, t)
+            for j in order:
+                strip(j, nrm_s, dv_s, slice(W, VC), 3)
+
+        @pl.when(i == 1)
+        def _():
+            close(1)
+            slot(2, 1)
 
         return carry
 
+    def rows_of(t, a):
+        return pl.ds((2 * t + a) * rows, rows)
+
+    def result(t, a):
+        out = (out_ref, gt_ref)[t].at[:, cols[a]]
+        return pltpu.make_async_copy(dsh_s.at[rows_of(t, a)], out, ls.at[2 * t + a])
+
+    for a in range(2):
+        seq_one(0, a, 1).wait_recv()
+        seq_two(0, a).wait_recv()
+        dsh_s[rows_of(0, a), :] = add(xc_s[mine, cols[a]], chunk(s, a)[...], ab0[a, 1], az0[a, 1])
+        result(0, a).start()
+    for j in order[:2]:
+        strip(j, nrm_s, dv_s, every, 2)
+    ends(2, range(1))
     lax.fori_loop(0, SEQ, dn_part, 0)
 
     conv_s[...] = jnp.zeros_like(conv_s)
@@ -1000,10 +1023,15 @@
 
     for k in range(1, nf):
         small_send(k).start()
+    ends(3, range(nl - 1))
+    for t in range(2, nl - 1):
+        slot(2, t)
     seq_pass(1)
-    for g in (2, 3):
-        for t in range(2, nl - 1):
-            slot(g, t)
+    relay(1)
+    close(2)
+    for t in range(1, nl - 1):
+        slot(3, t)
+
     total = snd_s[f]
     for k in range(1, nf):
         small_send(k).wait_recv()
@@ -1015,27 +1043,31 @@
 
     for k in range(1, SEQ):
         small_share(k).start()
-    close(2)
     close(3)
     relay(2)
-    relay(3)
 
     for a in range(2):
         seq_one(1, a, 1).wait_recv()
         seq_two(1, a).wait_recv()
-        gt_ref[:, cols[a]] = add(chunk(s, a)[...], ab1[a, 1], az1[a, 1])
+        dsh_s[rows_of(1, a), :] = add(chunk(s, a)[...], ab1[a, 1], az1[a, 1])
 
     def grad_tokens(i, carry):
-        r = pl.ds(pl.multiple_of(i * 64, 64), 64)
         x = xc_s[pl.ds(pl.multiple_of(s * rows + i * 64, 64), 64), :].astype(F32)
         rho = lax.rsqrt(jnp.sum(x * x, axis=1, keepdims=True) * (1.0 / D) + EPS)
-        n0 = x * rho
-        e0 = gt_ref[r, :] * pre_s[5:6, :]
-        mean = jnp.sum(e0 * n0, axis=1, keepdims=True) * (1.0 / D)
-        gt_ref[r, :] = cotrow_s[r, :].astype(F32) + rho * (e0 - n0 * mean)
+        at = [pl.ds(pl.multiple_of((2 + a) * rows + i * 64, 64), 64) for a in range(2)]
+        n0 = [x[:, cols[a]] * rho for a in range(2)]
+        e0 = [dsh_s[at[a], :] * pre_s[5:6, cols[a]] for a in range(2)]
+        dot = sum(jnp.sum(e0[a] * n0[a], axis=1, keepdims=True) for a in range(2))
+        mean = dot * (1.0 / D)
+        cot = cotrow_s[pl.ds(pl.multiple_of(i * 64, 64), 64), :].astype(F32)
+        for a in range(2):
+            dsh_s[at[a], :] = cot[:, cols[a]] + rho * (e0[a] - n0[a] * mean)
         return carry
 
     lax.fori_loop(0, rows // 64, grad_tokens, 0)
+    for a in range(2):
+        result(1, a).start()
+    relay(3)
 
     for k in range(1, SEQ):
         small_share(k).wait()
@@ -1043,9 +1075,15 @@
     for k in range(SEQ):
         total = total + jnp.where(s == k, sown_s[...], sgot_s[k])
     small_ref[...] = total
+    for t in range(2):
+        for a in range(2):
+            result(t, a).wait()
     for k in range(1, nf):
         small_send(k).wait_send()
-    seq_sent(1)
+    seq_one_sent(1)
+    for t in range(2):
+        for a in range(2):
+            seq_two(t, a).wait_send()
     for g in range(4):
         seq_gather_finish(g, owns[g], gouts[g], as_, ar, px, py, s)
         pltpu.make_async_copy(owns[g], gouts[g].at[pl.ds(s * n, n)], os_.at[g]).wait()
@@ -1069,7 +1107,7 @@
         functools.partial(back_kernel, nf),
         out_shape=[shape((rows, D), F32)] * 2 + [shape((SEQ * n, w), BF16) for w in widths] + [shape((8, 512), F32)],
         in_specs=[ANY] * len(big) + [VMEM] * len(par),
-        out_specs=[VMEM] * 2 + [ANY] * 4 + [VMEM],
+        out_specs=[ANY] * 6 + [VMEM],
         scratch_shapes=[
             vm((length, D), BF16),
             vm((length, D), BF16),
@@ -1131,8 +1169,69 @@
     )(*big, *par)
 
 
-def own_rows(array, index, row_count):
-    return lax.dynamic_slice_in_dim(array, index * row_count, row_count, 0)
+def finish_kernel(
+    go, gg, gv, gs, out, gt, small, out_o, gt_o, gin_o, gout_o, cw_o, cb_o, pre_o, post_o, step_o, decay_o, skip_o
+):
+    out_o[...] = out[...]
+    gt_o[...] = gt[...]
+    for i in range(SEQ):
+        gin_o[:, i * W : i * W + W] = gg[i].astype(F32)
+        gin_o[:, INNER + i * W : INNER + i * W + W] = gv[i].astype(F32)
+    total = gs[0].astype(F32)
+    for i in range(1, SEQ):
+        total = total + gs[i].astype(F32)
+    rest = gin_o.shape[1] - 2 * INNER
+    gin_o[:, 2 * INNER :] = total[:, :rest]
+    gout_o[...] = go[0].astype(F32)
+
+    @pl.when(pl.program_id(0) == 0)
+    def _():
+        cw_o[...] = small[0:4, : cw_o.shape[1]]
+        cb_o[...] = small[4:5, : cb_o.shape[1]]
+        pre_o[...] = small[5:6, : pre_o.shape[1]]
+        post_o[...] = small[6:7, : post_o.shape[1]]
+        heads = step_o.shape[1]
+        step_o[...] = small[7:8, :heads]
+        decay_o[...] = small[7:8, 128 : 128 + heads]
+        skip_o[...] = small[7:8, 256 : 256 + heads]
+
+
+def finish(nf, go, gg, gv, gs, out, gt, small):
+    shape = jax.ShapeDtypeStruct
+    n = D // nf
+    step, rows = n // SEQ, out.shape[0] // SEQ
+    proj = 2 * INNER + 2 * STATE + HEADS
+    go, gg, gv, gs = (g.reshape(SEQ, n, g.shape[1]) for g in (go, gg, gv, gs))
+
+    def whole(*dims):
+        return pl.BlockSpec(dims, lambda i: (0,) * len(dims))
+
+    tiny = [(4, XBC // nf), (1, XBC // nf), (1, n), (1, INNER // nf)] + [(1, HEADS // nf)] * 3
+    return pl.pallas_call(
+        finish_kernel,
+        grid=(SEQ,),
+        out_shape=[shape(out.shape, F32)] * 2
+        + [shape((n, proj), F32), shape((n, INNER), F32)]
+        + [shape(dims, F32) for dims in tiny],
+        in_specs=[
+            pl.BlockSpec((1, n, W), lambda i: (i, 0, 0)),
+            pl.BlockSpec((SEQ, step, W), lambda i: (0, i, 0)),
+            pl.BlockSpec((SEQ, step, W), lambda i: (0, i, 0)),
+            pl.BlockSpec((SEQ, step, VC - W), lambda i: (0, i, 0)),
+            pl.BlockSpec((rows, D), lambda i: (i, 0)),
+            pl.BlockSpec((rows, D), lambda i: (i, 0)),
+            whole(8, 512),
+        ],
+        out_specs=[
+            pl.BlockSpec((rows, D), lambda i: (i, 0)),
+            pl.BlockSpec((rows, D), lambda i: (i, 0)),
+            pl.BlockSpec((step, proj), lambda i: (i, 0)),
+            pl.BlockSpec((n, W), lambda i: (0, i)),
+        ]
+        + [whole(*dims) for dims in tiny],
+        name="finish",
+        compiler_params=pltpu.CompilerParams(vmem_limit_bytes=VMEM_LIMIT),
+    )(go, gg, gv, gs, out, gt, small)
 
 
 def body(
@@ -1149,65 +1248,38 @@
     cotangent,
 ):
     nf = lax.axis_size("fsdp")
-    s = lax.axis_index("seq")
     tok = tokens.reshape(tokens.shape[1:])
     cot = cotangent.reshape(cotangent.shape[1:])
     win = input_projection_weight
-    n = win.shape[0]
-
-    w_state = jnp.concatenate(
-        [
-            win[:, 2 * INNER : 2 * INNER + 2 * STATE],
-            lax.dynamic_slice(win, (0, 2 * INNER + 2 * STATE + s * HL), (n, HL)),
-            jnp.zeros((n, 128 - HL), BF16),
-        ],
-        axis=1,
+
+    w_state = jnp.pad(win[:, 2 * INNER :], ((0, 0), (0, VC - W - (win.shape[1] - 2 * INNER))))
+    w_out = output_projection_weight.T
+
+    flat, at = jnp.zeros((2048,), F32), 0
+    for v, size in (
+        (conv_bias, 512), (pre_gain, 512), (post_gain, 512), (step_bias, 128), (decay_log, 128), (skip_gain, 256),
+    ):
+        flat = flat + jnp.pad(v.astype(F32), (at, 2048 - at - v.shape[0]))
+        at += size
+    taps = jnp.pad(conv_weight.T.astype(F32), ((0, 4), (0, 512 - conv_weight.shape[0])))
+    small = taps + jnp.pad(flat.reshape(4, 512), ((4, 0), (0, 0)))
+    outs = front(nf, tok, cot, win, w_state, w_out, small)
+    out, gt, g_out, g_gate, g_val, g_state, small = back(nf, outs[:12], outs[12:])
+    block_out, grad_tokens, grad_in, grad_out, cw, cb, pre, post, step, decay, skip = finish(
+        nf, g_out, g_gate, g_val, g_state, out, gt, small
     )
-    w_out = own_rows(output_projection_weight, s, W).T
-
-    def line(*pieces):
-        return jnp.concatenate([jnp.pad(v[None], ((0, 0), (0, 128 * t - v.shape[0]))) for v, t in pieces], axis=1)
-
-    small = jnp.concatenate(
-        [
-            jnp.pad(conv_weight.T, ((0, 0), (0, 512 - conv_weight.shape[0]))),
-            line((conv_bias, 4)),
-            line((pre_gain, 4)),
-            line((post_gain, 4)),
-            line((step_bias, 1), (decay_log, 1), (skip_gain, 2)),
-        ]
-    ).astype(F32)
-    outs = front(nf, tok, cot, win, w_state, w_out, small)
-    block_out, grad_tokens, g_out, g_gate, g_val, g_state, small = back(nf, outs[:12], outs[12:])
-
-    g_gate = g_gate.reshape(SEQ, n, W).astype(F32)
-    g_val = g_val.reshape(SEQ, n, W).astype(F32)
-    g_state = g_state.reshape(SEQ, n, VC - W).astype(F32)
-    grad_in = jnp.concatenate(
-        [g_gate[i] for i in range(SEQ)]
-        + [g_val[i] for i in range(SEQ)]
-        + [jnp.sum(g_state[:, :, : 2 * STATE], axis=0)]
-        + [g_state[i, :, 2 * STATE : 2 * STATE + HL] for i in range(SEQ)],
-        axis=1,
-    )
-    grad_out = jnp.swapaxes(g_out.reshape(SEQ, n, W), 1, 2).reshape(INNER, n).astype(F32)
-    nc = XBC // nf
-    nh = HEADS // nf
-    grad_cw, grad_cb = small[:4, :nc].T, small[4, :nc]
-    grad_pre, grad_post = small[5, :n], small[6, : INNER // nf]
-    grad_step, grad_decay, grad_skip = [small[7, 128 * i : 128 * i + nh] for i in range(3)]
     return (
         block_out[None],
         grad_tokens[None],
         grad_in,
-        grad_pre,
-        grad_cw,
-        grad_cb,
-        grad_step,
-        grad_decay,
-        grad_skip,
-        grad_post,
-        grad_out,
+        pre.reshape(-1),
+        cw.T,
+        cb.reshape(-1),
+        step.reshape(-1),
+        decay.reshape(-1),
+        skip.reshape(-1),
+        post.reshape(-1),
+        grad_out.T,
     )
 
 

time: 241 us -> 212 us (0.88)
  local copies, waits for them, and re-layouts: 26.7 us -> 1.62 us
    pallas_call x1, Pallas kernels: 88.6 us -> 74.3 us  [front(): pl.pallas_call(functools.partial(front_kernel, nf), out_shape=big + par,...]
    pallas_call x0 -> x1, Pallas kernels: none -> 7.25 us  [finish(): pl.pallas_call(finish_kernel, grid=(SEQ,), out_shape=[shape(out.shape, F3...]
    concatenate x3 -> x0, local copies, waits for them, and re-layouts: 5.44 us -> none  [the longest x1 5.33 us: body(): jnp.concatenate([g_gate[i] for i in range(SEQ)] + [g_val[i] for i in rang...]
    slice x5 -> x1, local copies, waits for them, and re-layouts: 6.2 us -> 0.92 us  [body(): win[:, 2 * INNER:]]
    unnamed x10 -> x0, local copies, waits for them, and re-layouts: 4.72 us -> none
    pallas_call x1, Pallas kernels: 118 us -> 122 us  [back(): pl.pallas_call(functools.partial(back_kernel, nf), out_shape=[shape((rows...]
    transpose x2 -> x0, local copies, waits for them, and re-layouts: 3.01 us -> none  [the longest x1 1.69 us: body(): w_out = own_rows(output_projection_weight, s, W).T]
where the time goes in v1:
time: 212 us; the launch traced here: 209 us
  Pallas kernels  204 us (96%)
  other arithmetic  3.3 us (2%)
    pallas_call x1, Pallas kernels, back(): pl.pallas_call(functools.partial(back_kernel, nf), out_shape=[shape((rows...  122 us
    pallas_call x1, Pallas kernels, front(): pl.pallas_call(functools.partial(front_kernel, nf), out_shape=big + par,...  74.3 us
    pallas_call x1, Pallas kernels, finish(): pl.pallas_call(finish_kernel, grid=(SEQ,), out_shape=[shape(out.shape, F3...  7.25 us

profile of v1, /device:TPU:8, one launch (start us, length us, event | category | flops | bytes accessed | tf_op | source)
XLA Modules:
  0.0 209.4 jit_solution(2240678491486370915)
XLA Ops:
  0.6 0.8 convert_add_fusion
  1.4 1.3 pad_add_fusion.small
  2.7 0.9 slice.3
  3.7 0.7 pad.57.wst
  4.3 74.3 %front.1 = (bf16[1024,1536]{1,0:T(8,128)(2,1)}, bf16[1024,1536]{1,0:T(8,128)(2,1)}, bf16[1024,1536]{1,0:T(8,128)(2,1)}, bf16[1536,768]{1,0:T(8,128)(2,1)}, bf16[...) custom-call(bf16[256,1536]{1,0:T(8,128)(2,1)} %bitcast.21, ...), custom_call_target="tpu_custom_call" | custom-call | tf_op jit(solution)/shard_map/front/pallas_call | solution.py:603
  78.7 122.2 %back.1 = (f32[256,1536]{1,0:T(8,128)}, f32[256,1536]{1,0:T(8,128)}, bf16[768,768]{1,0:T(8,128)(2,1)}, bf16[768,768]{1,0:T(8,128)(2,1)}, bf16[768,768]{1,0:T(8,1...) custom-call(bf16[1024,1536]{1,0:T(8,128)(2,1)} %get-tuple-element.46.x_in, ...), custom_call_target="tpu_custom_call" | custom-call | tf_op jit(solution)/shard_map/back/pallas_call | solution.py:1106
  200.9 7.3 %finish.1 = (f32[256,1536]{1,0:T(8,128)}, f32[256,1536]{1,0:T(8,128)}, f32[192,6448]{1,0:T(8,128)}, f32[192,3072]{1,0:T(8,128)}, f32[4,416]{1,0:T(4,128)}, /*ind...) custom-call(bf16[4,192,768]{2,1,0:T(8,128)(2,1)} %bitcast.17, ...), custom_call_target="tpu_custom_call" | custom-call | tf_op jit(solution)/shard_map/finish/pallas_call | solution.py:1210
  208.2 1.2 reduce
  (1 shorter events, 0.0 us)

commit v2 on v1

--- a/solution.py
+++ b/solution.py
@@ -293,15 +293,36 @@
     return start, lanes, block
 
 
-def front_kernel(
+TN = (((0,), (0,)), ((), ()))
+STRIP = 384
+
+
+def unplace(block, at, width):
+    start, shift = at // 128 * 128, at % 128
+    lanes = -(-(width + shift) // 128) * 128
+    piece = block[:, start : start + lanes]
+    if shift:
+        piece = pltpu.roll(piece, lanes - shift, 1)
+    if lanes < 512:
+        piece = jnp.concatenate([piece, jnp.zeros((piece.shape[0], 512 - lanes), piece.dtype)], axis=1)
+    else:
+        piece = piece[:, :512]
+    return jnp.where(lax.broadcasted_iota(jnp.int32, piece.shape, 1) < width, piece, 0.0)
+
+
+def mixer_kernel(
     nf, tok, cot, win, wst, wout, small,
-    x_out, cot_out, nrm_out, wv_out, ws_out, wg_out, wo_out, mix_out, gate_out, mixed_out, st_out, dsh_out,
-    kw_s, hp_s, ex_s, pre_s, stat_s,
-    x_s, cot_s, nrm_s, wv_s, ws_s, wg_s, wo_s, mix_s, gate_s, mixed_s, st_s, dsh_s,
-    small_s, conv_s, post_s, stat_own, stat_got,
-    buf, hst, xw_s, er_s,
-    xs, xr, zs, zr, ms, mr, es, er, ls, os_,
+    out_ref, gt_ref, go_ref, gg_ref, gv_ref, gs_ref, small_ref, x_hbm,
+    cot_s, nrm_s, wv_s, ws_s, wg_s, wo_s, mix_s, gate_s, mixed_s, st_s, dsh_s,
+    dy_s, dv_s, cotrow_s, part_s, ga_s, gb_s, gc_s,
+    pb0, pb1, pb2, pb3, pb4, lb0, lb1, lb2, lb3, lb4, own0, own1, own2, own3, own4,
+    ab0, ab1, az0, az1,
+    kw_s, hp_s, ex_s, pre_s, stat_s, stat_own, stat_got,
+    gcw_s, gch_s, ghd_s, gpost_s, gpre_s, conv_s, post_s, snd_s, got_s, sown_s, sgot_s,
+    buf, cbuf, dhst, rowp, xw_s, e_s, er_s,
+    ls, xs, xr, zs, zr, ms, mr, es, er, bzs, bzr, bxs, bxr, as_, ar, bms, bmr, bes, ber, os_,
 ):
+    x_s, small_s = part_s, snd_s
     s = lax.axis_index("seq")
     f = lax.axis_index("fsdp")
     px, py = s ^ 1, s ^ 2
@@ -318,16 +339,17 @@
     n = win.shape[0]
     rows = tok.shape[0]
     length = rows * SEQ
+    quarter = n // SEQ
     ins = (
         win.at[:, pl.ds(pl.multiple_of(INNER + s * W, 128), W)],
-        wst,
+        wst.at[pl.ds(pl.multiple_of(s * quarter, 8), quarter)],
         win.at[:, pl.ds(pl.multiple_of(s * W, 128), W)],
         wout.at[:, pl.ds(pl.multiple_of(s * W, 128), W)],
     )
     outs = (wv_s, ws_s, wg_s, wo_s)
 
     def row(g, i):
-        return outs[g].at[pl.ds(i * n, n)]
+        return ws_s.at[i, s] if g == 1 else outs[g].at[pl.ds(i * n, n)]
 
     def hop(g, src, i, way, k, device):
         return rcopy(src, row(g, i), zs.at[g, way, k], zr.at[g, i], {"fsdp": device})
@@ -412,21 +434,36 @@
     own_small = pltpu.make_async_copy(small, small_s.at[f], ls.at[4])
     own_tok = pltpu.make_async_copy(tok, x_s.at[mine], ls.at[5])
     own_cot = pltpu.make_async_copy(cot, cot_s.at[mine], ls.at[6])
+    own_row = pltpu.make_async_copy(cot, cotrow_s, ls.at[7])
+
+    def st_hop(k, region, device):
+        return rcopy(region, region, xs.at[2, k], xr.at[2, k], {"seq": device})
+
+    st_own = ws_s.at[:, s]
+    st_top, st_low = ws_s.at[pl.ds(0, nl), px], ws_s.at[pl.ds(nl, nl), py]
 
     for k in range(1, nf):
         small_copy(k).start()
     own_small.start()
     own_tok.start()
     seq_gather_start((tok,), (x_s,), xs, xr, px, py, s)
+    own_send(1)
     own_send(0)
-    own_send(1)
     own_cot.start()
+    own_row.start()
+    for k in range(1, min(3, nl)):
+        step(1, k)
     step(0, 1)
-    step(1, 1)
+    for k in range(3, nl):
+        step(1, k)
+    arrive(1)
+    st_hop(0, st_own, px).start()
+    st_hop(1, st_own, py).start()
     seq_gather_relay(0, tok, x_s, xs, xr, px, py, s)
-    own = cot_s.at[mine]
-    rcopy(cot, own, xs.at[1, 0], xr.at[1, 0], {"seq": px}).start()
-    rcopy(cot, own, xs.at[1, 1], xr.at[1, 1], {"seq": py}).start()
+    for k in range(2, min(3, nl)):
+        step(0, k)
+    own_send(2)
+    own_send(3)
 
     own_small.wait()
     for k in range(1, nf):
@@ -461,15 +498,15 @@
         ex_s[0:1, 128 * i : 128 * i + 128] = jnp.where(low1, spread(skip, 2 * i), spread(skip, 2 * i + 1))
     ex_s[1:2, :] = post_s[6:7, pl.ds(pl.multiple_of(s * W, 128), W)]
 
-    for k in range(2, nl):
+    st_hop(0, st_own, px).wait_recv()
+    st_hop(2, st_top, py).start()
+    st_hop(1, st_own, py).wait_recv()
+    st_hop(3, st_low, px).start()
+    own = cot_s.at[mine]
+    rcopy(cot, own, xs.at[1, 0], xr.at[1, 0], {"seq": px}).start()
+    rcopy(cot, own, xs.at[1, 1], xr.at[1, 1], {"seq": py}).start()
+    for k in range(3, nl):
         step(0, k)
-        step(1, k)
-        if k == 2:
-            own_send(2)
-            own_send(3)
-    if nl < 3:
-        own_send(2)
-        own_send(3)
     own_tok.wait()
     seq_gather_finish(0, tok, x_s, xs, xr, px, py, s)
 
@@ -481,57 +518,44 @@
         return carry
 
     lax.fori_loop(0, length // 128, norm, 0)
+    x_save = pltpu.make_async_copy(x_s, x_hbm, ls.at[8])
+    x_save.start()
     arrive(0)
-    arrive(1)
-
-    saves = [
-        pltpu.make_async_copy(a, b, os_.at[i])
-        for i, (a, b) in enumerate(
-            (
-                (x_s, x_out), (cot_s, cot_out), (nrm_s, nrm_out), (wv_s, wv_out), (ws_s, ws_out), (wg_s, wg_out),
-                (wo_s, wo_out), (mix_s, mix_out), (gate_s, gate_out), (mixed_s, mixed_out), (st_s, st_out),
-                (dsh_s, dsh_out),
-            )
-        )
-    ]
-    for i in (0, 2, 3, 4):
-        saves[i].start()
 
     def project(i, carry):
         r = pl.ds(pl.multiple_of(i * 256, 256), 256)
-        a = nrm_s[r, :]
-        mix_s[r, 0:W] = nn(a, wv_s[...]).astype(BF16)
-        mix_s[r, W:VC] = nn(a, ws_s[...]).astype(BF16)
+        mix_s[r, 0:W] = nn(nrm_s[r, :], wv_s[...]).astype(BF16)
+        return carry
+
+    def project_state(i, carry):
+        r = pl.ds(pl.multiple_of(i * 256, 256), 256)
+        mix_s[r, W:VC] = nn(nrm_s[r, :], ws_s[...].reshape(D, VC - W)).astype(BF16)
         return carry
 
     lax.fori_loop(0, length // 256, project, 0)
     step(2, 1)
-    saves[7].start()
+    st_hop(2, st_top, py).wait()
+    st_hop(3, st_low, px).wait()
+    lax.fori_loop(0, length // 256, project_state, 0)
 
     def between(b):
         @pl.when(b == 1)
         def _():
-            seq_gather_relay(1, cot, cot_s, xs, xr, px, py, s)
-
-        @pl.when(b == 2)
-        def _():
             step(3, 1)
 
-        @pl.when(b == 5)
+        @pl.when(b == 4)
         def _():
             step(2, 2)
 
     scan_fwd_blocks(
         mix_s.at[:, 0:W], mix_s.at[:, W:CH], mix_s.at[:, CH:VC], kw_s, hp_s, ex_s, mixed_s, st_s,
-        buf, hst, xw_s, er_s, between,
+        buf, dhst, xw_s, er_s, between,
     )
-    for i in (9, 10):
-        saves[i].start()
     step(3, 2)
+    seq_gather_relay(1, cot, cot_s, xs, xr, px, py, s)
     for k in range(3, nl):
         step(2, k)
     arrive(2)
-    saves[5].start()
 
     def project_gate(i, carry):
         r = pl.ds(pl.multiple_of(i * 256, 256), 256)
@@ -539,14 +563,11 @@
         return carry
 
     lax.fori_loop(0, length // 256, project_gate, 0)
-    saves[8].start()
     for k in range(3, nl):
         step(3, k)
     own_cot.wait()
     seq_gather_finish(1, cot, cot_s, xs, xr, px, py, s)
-    saves[1].start()
     arrive(3)
-    saves[6].start()
     eye = lax.broadcasted_iota(jnp.int32, (128, 128), 0) == lax.broadcasted_iota(jnp.int32, (128, 128), 1)
 
     def stats(i, carry):
@@ -562,7 +583,6 @@
         return carry
 
     lax.fori_loop(0, length // 128, stats, 0)
-    saves[11].start()
     copies = [rcopy(stat_own, stat_got.at[k], es.at[k], er.at[k], {"seq": s ^ k}) for k in range(1, SEQ)]
     for copy in copies:
         copy.start()
@@ -571,127 +591,9 @@
     stat_s[...] = stat_own[...] + stat_got[1] + (stat_got[2] + stat_got[3])
     for g in range(GROUPS):
         sent(g)
-    for save in saves:
-        save.wait()
-
-
-def front(nf, tok, cot, win, wst, wout, small):
-    shape = jax.ShapeDtypeStruct
-    dma = pltpu.SemaphoreType.DMA
-    length = SEQ * tok.shape[0]
-    big = [
-        shape((length, D), BF16),
-        shape((length, D), BF16),
-        shape((length, D), BF16),
-        shape((D, W), BF16),
-        shape((D, VC - W), BF16),
-        shape((D, W), BF16),
-        shape((D, W), BF16),
-        shape((length, VC), BF16),
-        shape((length, W), BF16),
-        shape((length, W), BF16),
-        shape((length // Q, STATE, W), BF16),
-        shape((length, W), F32),
-    ]
-    par = [
-        shape((8, CH), F32),
-        shape((8, 128), F32),
-        shape((8, W), F32),
-        shape((8, D), F32),
-        shape((2 * length // 128, 128), F32),
-    ]
-    return pl.pallas_call(
-        functools.partial(front_kernel, nf),
-        out_shape=big + par,
-        in_specs=[ANY] * 5 + [VMEM],
-        out_specs=[ANY] * len(big) + [VMEM] * len(par),
-        scratch_shapes=[pltpu.VMEM(b.shape, b.dtype) for b in big]
-        + [
-            pltpu.VMEM((nf, 8, 512), F32),
-            pltpu.VMEM((8, XBC), F32),
-            pltpu.VMEM((8, INNER), F32),
-            pltpu.VMEM((2 * length // 128, 128), F32),
-            pltpu.VMEM((SEQ, 2 * length // 128, 128), F32),
-            pltpu.VMEM((Q + 8, CH), F32),
-            pltpu.VMEM((STATE, W), F32),
-            pltpu.VMEM((Q, W), BF16),
-            pltpu.VMEM((8, W), F32),
-            dma((2, 4)),
-            dma((2, 4)),
-            dma((GROUPS, 4, nf // 2)),
-            dma((GROUPS, nf)),
-            dma((nf,)),
-            dma((nf,)),
-            dma((SEQ,)),
-            dma((SEQ,)),
-            dma((7,)),
-            dma((len(big),)),
-        ],
-        name="front",
-        compiler_params=pltpu.CompilerParams(
-            collective_id=1, has_side_effects=True, vmem_limit_bytes=VMEM_LIMIT
-        ),
-    )(tok, cot, win, wst, wout, small)
-
-
-TN = (((0,), (0,)), ((), ()))
-STRIP = 384
-
-
-def unplace(block, at, width):
-    start, shift = at // 128 * 128, at % 128
-    lanes = -(-(width + shift) // 128) * 128
-    piece = block[:, start : start + lanes]
-    if shift:
-        piece = pltpu.roll(piece, lanes - shift, 1)
-    if lanes < 512:
-        piece = jnp.concatenate([piece, jnp.zeros((piece.shape[0], 512 - lanes), piece.dtype)], axis=1)
-    else:
-        piece = piece[:, :512]
-    return jnp.where(lax.broadcasted_iota(jnp.int32, piece.shape, 1) < width, piece, 0.0)
-
-
-def back_kernel(
-    nf, x_in, cot_in, nrm_in, wv_in, ws_in, wg_in, wo_in, mix_in, gate_in, mixed_in, st_in, dsh_in,
-    kw_s, hp_s, ex_s, pre_s, stat_s,
-    out_ref, gt_ref, go_ref, gg_ref, gv_ref, gs_ref, small_ref,
-    xc_s, nrm_s, wv_s, ws_s, wg_s, wo_s, mix_s, gate_s, mixed_s, st_s, dsh_s,
-    dy_s, dv_s, cotrow_s, part_s, ga_s, gb_s, gc_s,
-    pb0, pb1, pb2, pb3, lb0, lb1, lb2, lb3, own0, own1, own2, own3,
-    ab0, ab1, az0, az1,
-    gcw_s, gch_s, ghd_s, gpost_s, gpre_s, conv_s, post_s, snd_s, got_s, sown_s, sgot_s,
-    buf, cbuf, dhst, rowp, xw_s, e_s, er_s,
-    ls, zs, zr, xs, xr, as_, ar, ms, mr, es, er, os_,
-):
-    s = lax.axis_index("seq")
-    f = lax.axis_index("fsdp")
-    px, py = s ^ 1, s ^ 2
-    nl = nf // 2
-    p, c = f // 2, f % 2
-    partner = p * 2 + 1 - c
-    bar = pltpu.get_barrier_semaphore()
-    for k in range(1, SEQ):
-        signal(bar, {"seq": s ^ k})
-    for k in range(1, nf):
-        signal(bar, {"fsdp": lax.rem(f + k, nf)})
-
-    length = nrm_s.shape[0]
-    rows = length // SEQ
-    n = D // nf
-    mine = pl.ds(s * rows, rows)
-    loads = [
-        pltpu.make_async_copy(a, b, ls.at[i])
-        for i, (a, b) in enumerate(
-            (
-                (gate_in, gate_s), (mixed_in, mixed_s), (dsh_in, dsh_s), (cot_in, xc_s), (wo_in, wo_s),
-                (nrm_in, nrm_s), (mix_in, mix_s), (st_in, st_s), (wg_in, wg_s), (wv_in, wv_s), (ws_in, ws_s),
-                (cot_in.at[mine], cotrow_s), (x_in, xc_s),
-            )
-        )
-    ]
-    for load in loads[:-1]:
-        load.start()
-    pl.semaphore_wait(bar, nf - 1 + SEQ - 1)
+    st_hop(0, st_own, px).wait_send()
+    st_hop(1, st_own, py).wait_send()
+    own_row.wait()
 
     half = D // 2
     cols = (slice(0, half), slice(half, D))
@@ -703,10 +605,10 @@
 
     def seq_one(t, a, m):
         i = (first[a] ^ second[a] ^ s) if m == 0 else first[a]
-        return rcopy(chunk(i, a), ab[t].at[a, m], xs.at[t, a, m], xr.at[t, a, m], {"seq": first[a]})
+        return rcopy(chunk(i, a), ab[t].at[a, m], bxs.at[t, a, m], bxr.at[t, a, m], {"seq": first[a]})
 
     def seq_two(t, a):
-        return rcopy(az[t].at[a, 0], az[t].at[a, 1], xs.at[t, a, 2], xr.at[t, a, 2], {"seq": second[a]})
+        return rcopy(az[t].at[a, 0], az[t].at[a, 1], bxs.at[t, a, 2], bxr.at[t, a, 2], {"seq": second[a]})
 
     def add(*terms):
         total = terms[0].astype(F32)
@@ -731,22 +633,23 @@
             seq_one(t, a, 0).wait_send()
             seq_one(t, a, 1).wait_send()
 
-    parts = (ga_s, gb_s, ga_s, gc_s)
-    pbs, lbs, owns = (pb0, pb1, pb2, pb3), (lb0, lb1, lb2, lb3), (own0, own1, own2, own3)
-    gouts = (go_ref, gg_ref, gv_ref, gs_ref)
+    low_half, high_half = slice(0, W // 2), slice(W // 2, W)
+    parts = (ga_s, gb_s, ga_s.at[:, low_half], ga_s.at[:, high_half], gc_s)
+    pbs, lbs, owns = (pb0, pb1, pb2, pb3, pb4), (lb0, lb1, lb2, lb3, lb4), (own0, own1, own2, own3, own4)
+    gouts = (go_ref, gg_ref, gv_ref.at[:, low_half], gv_ref.at[:, high_half], gs_ref)
 
     def piece(g, i):
         return parts[g].at[pl.ds(pl.multiple_of(i * n, 16), n)]
 
     def swap(g, q):
-        return rcopy(piece(g, q * 2 + 1 - c), pbs[g].at[q], zs.at[g, 0, q], zr.at[g, 0, q], {"fsdp": partner})
+        return rcopy(piece(g, q * 2 + 1 - c), pbs[g].at[q], bzs.at[g, 0, q], bzr.at[g, 0, q], {"fsdp": partner})
 
     def up(g, q):
-        return rcopy(pbs[g].at[q], lbs[g].at[q], zs.at[g, 1, q], zr.at[g, 1, q], {"fsdp": f + 2})
+        return rcopy(pbs[g].at[q], lbs[g].at[q], bzs.at[g, 1, q], bzr.at[g, 1, q], {"fsdp": f + 2})
 
     def down(g, q):
         to = jnp.where(q == p - 1, nl, q)
-        return rcopy(pbs[g].at[q], lbs[g].at[to], zs.at[g, 2, q], zr.at[g, 2, q], {"fsdp": f - 2})
+        return rcopy(pbs[g].at[q], lbs[g].at[to], bzs.at[g, 2, q], bzr.at[g, 2, q], {"fsdp": f - 2})
 
     def send_up(g, q, terms):
         pbs[g][q] = add(piece(g, q * 2 + c)[...], pbs[g][q], *terms).astype(BF16)
@@ -832,16 +735,14 @@
     for k in range(D // STRIP // 2):
         order += [D // STRIP - 1 - k, k]
 
-    def strip(j, a_ref, b_ref, bcols, g):
+    def strip(j, a_ref, b_ref, bcols, to, groups):
         at = slice(j * STRIP, (j + 1) * STRIP)
-        parts[g][at, :] = lax.dot_general(a_ref[:, at], b_ref[:, bcols], TN, preferred_element_type=F32).astype(BF16)
+        to[at, :] = lax.dot_general(a_ref[:, at], b_ref[:, bcols], TN, preferred_element_type=F32).astype(BF16)
         for q in range(nl):
             if j * STRIP <= q * 2 * n < (j + 1) * STRIP:
-                swap(g, q).start()
-
-    for i in range(3):
-        loads[i].wait()
-    eye = lax.broadcasted_iota(jnp.int32, (128, 128), 0) == lax.broadcasted_iota(jnp.int32, (128, 128), 1)
+                for g in groups:
+                    swap(g, q).start()
+
     gpost_s[...] = jnp.zeros_like(gpost_s)
 
     def gated_norm(i, carry):
@@ -867,7 +768,12 @@
     lax.fori_loop(0, length // 128, gated_norm, 0)
 
     every = slice(0, W)
-    loads[4].wait()
+    for j in order:
+        strip(j, cot_s, mixed_s, every, ga_s, (0,))
+    ends(0, range(nl // 2))
+    x_save.wait()
+    x_load = pltpu.make_async_copy(x_hbm, cot_s, ls.at[8])
+    x_load.start()
 
     def out_part(i, carry):
         r = pl.ds(pl.multiple_of((s ^ (SEQ - 1 - i)) * rows, rows), rows)
@@ -886,105 +792,115 @@
         return carry
 
     lax.fori_loop(0, SEQ, out_part, 0)
-    loads[3].wait()
+
+    def rows_of(t, a):
+        return pl.ds((2 * t + a) * rows, rows)
+
+    def result(t, a):
+        out = (out_ref, gt_ref)[t].at[:, cols[a]]
+        return pltpu.make_async_copy(dsh_s.at[rows_of(t, a)], out, ls.at[2 * t + a])
+
+    for a in range(2):
+        dsh_s[rows_of(0, a), :] = chunk(s, a)[...].astype(F32)
+
     for j in order:
-        strip(j, xc_s, mixed_s, every, 0)
-    loads[-1].start()
-    ends(0, range(nl - 1))
-
-    loads[5].wait()
-    for j in order:
-        strip(j, nrm_s, gate_s, every, 1)
-    ends(1, range(nl - 1))
-    loads[6].wait()
-    loads[7].wait()
+        strip(j, nrm_s, gate_s, every, gb_s, (1,))
+    ends(1, range(nl // 2))
+    ends(0, range(nl // 2, nl - 1))
+    ends(1, range(nl // 2, nl - 1))
+    slot(0, 1)
+
+    gpre_s[...] = jnp.zeros_like(gpre_s)
+
+    def dn_chunk(j):
+        r = pl.ds(pl.multiple_of(j * rows, rows), rows)
+        dn = nt(gate_s[r, :], wg_s[...]) + nt(dv_s[r, 0:W], wv_s[...])
+        dn = dn + nt(dv_s[r, W:VC], ws_s[...].reshape(D, VC - W))
+        part_s[r, :] = dn.astype(BF16)
+        x = cot_s[r, :].astype(F32)
+        rho = lax.rsqrt(jnp.sum(x * x, axis=1, keepdims=True) * (1.0 / D) + EPS)
+        gpre_s[5:6, :] += jnp.sum(dn * (x * rho), axis=0, keepdims=True)
+
+        @pl.when((s ^ j) == 3)
+        def _():
+            seq_one(1, 0, 0).start()
+            seq_one(1, 1, 0).start()
+
+        @pl.when((s ^ j) == 1)
+        def _():
+            seq_one(1, 0, 1).start()
+
+        @pl.when((s ^ j) == 2)
+        def _():
+            seq_one(1, 1, 1).start()
+
+    def dn_pass(j):
+        for a in range(2):
+            @pl.when((s ^ j) == 2 - a)
+            def _():
+                seq_one(1, a, 0).wait_recv()
+                az1[a, 0] = add(chunk(second[a], a)[...], ab1[a, 0]).astype(BF16)
+                seq_two(1, a).start()
 
     def between(i):
-        @pl.when(i == 0)
-        def _():
-            slot(0, 1)
-
         @pl.when(i == 1)
         def _():
             seq_pass(0)
-
-        @pl.when(i == 2)
+            seq_one_sent(0)
+            x_load.wait()
+
+        @pl.when(jnp.logical_or(i == 1, i == 3))
+        def _():
+            dn_chunk(SEQ - 1 - i // 2)
+
+        @pl.when(i == 1)
         def _():
             for t in range(2, nl - 1):
                 slot(0, t)
 
-        @pl.when(i == 3)
-        def _():
-            close(0)
+        @pl.when(i == 2)
+        def _():
+            slot(1, 1)
 
         @pl.when(i == 4)
-        def _():
-            slot(1, 1)
-
-        @pl.when(i == 6)
         def _():
             for t in range(2, nl - 1):
                 slot(1, t)
-            relay(0)
+            close(0)
+
+        @pl.when(i == 5)
+        def _():
+            dn_pass(3)
+
+        @pl.when(i == 6)
+        def _():
+            close(1)
 
     scan_bwd_blocks(
         mix_s.at[:, 0:W], mix_s.at[:, W:CH], mix_s.at[:, CH:VC], dy_s, st_s, kw_s, hp_s, ex_s,
         dv_s, gcw_s, gch_s, ghd_s, buf, cbuf, dhst, rowp, xw_s, e_s, er_s, between,
     )
 
-    loads[-1].wait()
     swaps_sent(0)
-    seq_one_sent(0)
-    for i in range(8, 12):
-        loads[i].wait()
-    gpre_s[...] = jnp.zeros_like(gpre_s)
-
-    def dn_part(i, carry):
-        r = pl.ds(pl.multiple_of((s ^ (SEQ - 1 - i)) * rows, rows), rows)
-        dn = nt(gate_s[r, :], wg_s[...]) + nt(dv_s[r, 0:W], wv_s[...]) + nt(dv_s[r, W:VC], ws_s[...])
-        part_s[r, :] = dn.astype(BF16)
-        x = xc_s[r, :].astype(F32)
-        rho = lax.rsqrt(jnp.sum(x * x, axis=1, keepdims=True) * (1.0 / D) + EPS)
-        gpre_s[5:6, :] += jnp.sum(dn * (x * rho), axis=0, keepdims=True)
-
-        @pl.when(i == 0)
-        def _():
-            for a in range(2):
-                seq_one(1, a, 0).start()
-            for j in order[2:]:
-                strip(j, nrm_s, dv_s, every, 2)
-            ends(2, range(1, nl - 1))
-
-        @pl.when(i == 2)
-        def _():
-            for a in range(2):
-                seq_one(1, a, 1).start()
-            for j in order:
-                strip(j, nrm_s, dv_s, slice(W, VC), 3)
-
-        @pl.when(i == 1)
-        def _():
-            close(1)
-            slot(2, 1)
-
-        return carry
-
-    def rows_of(t, a):
-        return pl.ds((2 * t + a) * rows, rows)
-
-    def result(t, a):
-        out = (out_ref, gt_ref)[t].at[:, cols[a]]
-        return pltpu.make_async_copy(dsh_s.at[rows_of(t, a)], out, ls.at[2 * t + a])
-
-    for a in range(2):
-        seq_one(0, a, 1).wait_recv()
-        seq_two(0, a).wait_recv()
-        dsh_s[rows_of(0, a), :] = add(xc_s[mine, cols[a]], chunk(s, a)[...], ab0[a, 1], az0[a, 1])
-        result(0, a).start()
     for j in order[:2]:
-        strip(j, nrm_s, dv_s, every, 2)
+        strip(j, nrm_s, dv_s, every, ga_s, (2, 3))
     ends(2, range(1))
-    lax.fori_loop(0, SEQ, dn_part, 0)
+    ends(3, range(1))
+    dn_chunk(0)
+    for j in order[2:]:
+        strip(j, nrm_s, dv_s, every, ga_s, (2, 3))
+    for k in range(1, nl - 1):
+        ends(2, (k,))
+        ends(3, (k,))
+    slot(2, 1)
+    dn_chunk(1)
+    slot(3, 1)
+    dn_pass(2)
+    relay(0)
+    for j in order:
+        strip(j, nrm_s, dv_s, slice(W, VC), gc_s, (4,))
+    for t in range(2, nl - 1):
+        slot(2, t)
 
     conv_s[...] = jnp.zeros_like(conv_s)
     conv_s[:, pl.ds(pl.multiple_of(s * W, 128), W)] = gcw_s[:, 0:W]
@@ -1019,18 +935,28 @@
 
     def small_send(k):
         to = lax.rem(f + k, nf)
-        return rcopy(snd_s.at[to], got_s.at[k], ms.at[k], mr.at[k], {"fsdp": to})
+        return rcopy(snd_s.at[to], got_s.at[k], bms.at[k], bmr.at[k], {"fsdp": to})
 
     for k in range(1, nf):
         small_send(k).start()
-    ends(3, range(nl - 1))
+    ends(4, range(nl - 1))
     for t in range(2, nl - 1):
-        slot(2, t)
-    seq_pass(1)
+        slot(3, t)
     relay(1)
+    dn_pass(0)
     close(2)
+    dn_pass(1)
+    close(3)
+
+    for a in range(2):
+        seq_one(0, a, 1).wait_recv()
+        seq_two(0, a).wait_recv()
+        at = rows_of(0, a)
+        dsh_s[at, :] = add(dsh_s[at, :], cot_s[mine, cols[a]], ab0[a, 1], az0[a, 1])
+        result(0, a).start()
+
     for t in range(1, nl - 1):
-        slot(3, t)
+        slot(4, t)
 
     total = snd_s[f]
     for k in range(1, nf):
@@ -1039,12 +965,13 @@
     sown_s[...] = total
 
     def small_share(k):
-        return rcopy(sown_s, sgot_s.at[s], es.at[k], er.at[k], {"seq": s ^ k})
+        return rcopy(sown_s, sgot_s.at[s], bes.at[k], ber.at[k], {"seq": s ^ k})
 
     for k in range(1, SEQ):
         small_share(k).start()
-    close(3)
     relay(2)
+    relay(3)
+    close(4)
 
     for a in range(2):
         seq_one(1, a, 1).wait_recv()
@@ -1052,7 +979,7 @@
         dsh_s[rows_of(1, a), :] = add(chunk(s, a)[...], ab1[a, 1], az1[a, 1])
 
     def grad_tokens(i, carry):
-        x = xc_s[pl.ds(pl.multiple_of(s * rows + i * 64, 64), 64), :].astype(F32)
+        x = cot_s[pl.ds(pl.multiple_of(s * rows + i * 64, 64), 64), :].astype(F32)
         rho = lax.rsqrt(jnp.sum(x * x, axis=1, keepdims=True) * (1.0 / D) + EPS)
         at = [pl.ds(pl.multiple_of((2 + a) * rows + i * 64, 64), 64) for a in range(2)]
         n0 = [x[:, cols[a]] * rho for a in range(2)]
@@ -1067,7 +994,7 @@
     lax.fori_loop(0, rows // 64, grad_tokens, 0)
     for a in range(2):
         result(1, a).start()
-    relay(3)
+    relay(4)
 
     for k in range(1, SEQ):
         small_share(k).wait()
@@ -1084,35 +1011,38 @@
     for t in range(2):
         for a in range(2):
             seq_two(t, a).wait_send()
-    for g in range(4):
+    for g in range(5):
         seq_gather_finish(g, owns[g], gouts[g], as_, ar, px, py, s)
         pltpu.make_async_copy(owns[g], gouts[g].at[pl.ds(s * n, n)], os_.at[g]).wait()
         line_sent(g)
-    for g in range(1, 4):
+    for g in range(1, 5):
         swaps_sent(g)
 
 
-def back(nf, big, par):
+def mixer(nf, tok, cot, win, wst, wout, small):
     shape = jax.ShapeDtypeStruct
     vm = pltpu.VMEM
     dma = pltpu.SemaphoreType.DMA
-    length = big[0].shape[0]
-    rows = length // SEQ
+    rows = tok.shape[0]
+    length = SEQ * rows
     nl = nf // 2
     n = D // nf
     widths = (W, W, W, VC - W)
-    boxes = [vm((nl, n, w), BF16) for w in widths] + [vm((nl + 1, n, w), BF16) for w in widths]
-    boxes += [vm((n, w), BF16) for w in widths]
+    groups = (W, W, W // 2, W // 2, VC - W)
+    boxes = [vm((nl, n, w), BF16) for w in groups] + [vm((nl + 1, n, w), BF16) for w in groups]
+    boxes += [vm((n, w), BF16) for w in groups]
     return pl.pallas_call(
-        functools.partial(back_kernel, nf),
-        out_shape=[shape((rows, D), F32)] * 2 + [shape((SEQ * n, w), BF16) for w in widths] + [shape((8, 512), F32)],
-        in_specs=[ANY] * len(big) + [VMEM] * len(par),
-        out_specs=[ANY] * 6 + [VMEM],
+        functools.partial(mixer_kernel, nf),
+        out_shape=[shape((rows, D), F32)] * 2
+        + [shape((SEQ * n, w), BF16) for w in widths]
+        + [shape((8, 512), F32), shape((length, D), BF16)],
+        in_specs=[ANY] * 5 + [VMEM],
+        out_specs=[ANY] * 6 + [VMEM, ANY],
         scratch_shapes=[
             vm((length, D), BF16),
             vm((length, D), BF16),
             vm((D, W), BF16),
-            vm((D, VC - W), BF16),
+            vm((nf, SEQ, n // SEQ, VC - W), BF16),
             vm((D, W), BF16),
             vm((D, W), BF16),
             vm((length, VC), BF16),
@@ -1132,6 +1062,13 @@
         + [vm((2, 2, rows, D // 2), BF16)] * 4
         + [
             vm((8, CH), F32),
+            vm((8, 128), F32),
+            vm((8, W), F32),
+            vm((8, D), F32),
+            vm((2 * length // 128, 128), F32),
+            vm((2 * length // 128, 128), F32),
+            vm((SEQ, 2 * length // 128, 128), F32),
+            vm((8, CH), F32),
             vm((8, W), F32),
             vm((8, 128), F32),
             vm((8, W), F32),
@@ -1149,24 +1086,32 @@
             vm((Q, W), BF16),
             vm((Q, W), BF16),
             vm((8, W), F32),
-            dma((13,)),
-            dma((4, 3, nl)),
-            dma((4, 3, nl)),
-            dma((2, 2, 3)),
-            dma((2, 2, 3)),
-            dma((4, 4)),
-            dma((4, 4)),
+            dma((9,)),
+            dma((3, 4)),
+            dma((3, 4)),
+            dma((GROUPS, 4, nl)),
+            dma((GROUPS, nf)),
             dma((nf,)),
             dma((nf,)),
             dma((SEQ,)),
             dma((SEQ,)),
-            dma((4,)),
+            dma((5, 3, nl)),
+            dma((5, 3, nl)),
+            dma((2, 2, 3)),
+            dma((2, 2, 3)),
+            dma((5, 4)),
+            dma((5, 4)),
+            dma((nf,)),
+            dma((nf,)),
+            dma((SEQ,)),
+            dma((SEQ,)),
+            dma((5,)),
         ],
-        name="back",
+        name="mixer",
         compiler_params=pltpu.CompilerParams(
-            collective_id=2, has_side_effects=True, vmem_limit_bytes=67043328
+            collective_id=1, has_side_effects=True, vmem_limit_bytes=67043328
         ),
-    )(*big, *par)
+    )(tok, cot, win, wst, wout, small)
 
 
 def finish_kernel(
@@ -1263,8 +1208,7 @@
         at += size
     taps = jnp.pad(conv_weight.T.astype(F32), ((0, 4), (0, 512 - conv_weight.shape[0])))
     small = taps + jnp.pad(flat.reshape(4, 512), ((4, 0), (0, 0)))
-    outs = front(nf, tok, cot, win, w_state, w_out, small)
-    out, gt, g_out, g_gate, g_val, g_state, small = back(nf, outs[:12], outs[12:])
+    out, gt, g_out, g_gate, g_val, g_state, small, _ = mixer(nf, tok, cot, win, w_state, w_out, small)
     block_out, grad_tokens, grad_in, grad_out, cw, cb, pre, post, step, decay, skip = finish(
         nf, g_out, g_gate, g_val, g_state, out, gt, small
     )

time: 212 us -> 204 us (0.962)
  Pallas kernels: 204 us -> 195 us
    pallas_call x2 -> x1, Pallas kernels: 197 us -> 188 us  [mixer(): pl.pallas_call(functools.partial(mixer_kernel, nf), out_shape=[shape((row...]
where the time goes in v2:
time: 204 us; the launch traced here: 201 us
  Pallas kernels  195 us (96%)
  other arithmetic  3.35 us (2%)
    pallas_call x1, Pallas kernels, mixer(): pl.pallas_call(functools.partial(mixer_kernel, nf), out_shape=[shape((row...  188 us
    pallas_call x1, Pallas kernels, finish(): pl.pallas_call(finish_kernel, grid=(SEQ,), out_shape=[shape(out.shape, F3...  7.25 us

profile of v2, /device:TPU:8, one launch (start us, length us, event | category | flops | bytes accessed | tf_op | source)
XLA Modules:
  0.0 201.0 jit_solution(12780505572354713299)
XLA Ops:
  0.6 0.8 convert_add_fusion
  1.4 1.3 pad_add_fusion.small
  2.7 0.9 slice.3
  3.7 0.7 pad.57.wst
  4.3 188.1 %mixer.1 = (f32[256,1536]{1,0:T(8,128)}, f32[256,1536]{1,0:T(8,128)}, bf16[768,768]{1,0:T(8,128)(2,1)}, bf16[768,768]{1,0:T(8,128)(2,1)}, bf16[768,768]{1,0:T(8,...) custom-call(bf16[256,1536]{1,0:T(8,128)(2,1)} %bitcast.21, ...), custom_call_target="tpu_custom_call" | custom-call | tf_op jit(solution)/shard_map/mixer/pallas_call | solution.py:1034
  192.5 7.3 %finish.1 = (f32[256,1536]{1,0:T(8,128)}, f32[256,1536]{1,0:T(8,128)}, f32[192,6448]{1,0:T(8,128)}, f32[192,3072]{1,0:T(8,128)}, f32[4,416]{1,0:T(4,128)}, /*ind...) custom-call(bf16[4,192,768]{2,1,0:T(8,128)(2,1)} %bitcast.17, ...), custom_call_target="tpu_custom_call" | custom-call | tf_op jit(solution)/shard_map/finish/pallas_call | solution.py:1155
  199.7 1.3 reduce
  (1 shorter events, 0.0 us)

commit v3 on v2

--- a/solution.py
+++ b/solution.py
@@ -85,7 +85,7 @@
 
 
 def sigmoid(x):
-    return 1.0 / (1.0 + jnp.exp(-x))
+    return 0.5 + 0.5 * jnp.tanh(0.5 * x)
 
 
 def rates_of(r_ref, rows, hp_ref, tri):
@@ -94,6 +94,10 @@
     dt = softplus(raw)
     lam = nn(tri, dt * hp_ref[1:2, :], HIGH)
     return raw, dt, lam
+
+
+def fold(x):
+    return jnp.sum(x.reshape(x.shape[0] // 8, 8, x.shape[1]), axis=0)
 
 
 def spread(mat, h):
@@ -220,8 +224,9 @@
                 lg = within * g
                 lgd = lg * dcol
                 daff_t = daff_t + lgd
-                col_n = jnp.where(lane == h, jnp.sum(aff_t * lg, axis=1, keepdims=True), col_n)
-                rowp[h : h + 1, :] = jnp.sum(aff_t * lgd, axis=0, keepdims=True)
+                pair = (aff_t * lg).astype(BF16)
+                col_n = col_n + nn(pair, jnp.where(lane == h, 1.0, 0.0).astype(BF16))
+                rowp[h : h + 1, :] = jnp.sum(pair.astype(F32) * dcol, axis=0, keepdims=True)
                 z.append(nn((aff_t * within).astype(BF16), dyb))
                 lc.append(lcol)
                 dc.append(dcol)
@@ -237,16 +242,16 @@
             re = e * ch[:, at]
             ci = xp * bdp * ew
             th = jnp.sum(dhst[:, at] * hb[:, at].astype(F32), axis=0, keepdims=True) * er_s[0:1, at]
+            heads = jnp.where(lane == 2 * i + jnp.where(row < HW, 0, 1), 1.0, 0.0).astype(BF16)
+            row_i = row_i + nn(re.astype(BF16), heads)
+            col_i = col_i + nn(ci.astype(BF16), heads)
             for h in (2 * i, 2 * i + 1):
-                mine = low if h % 2 == 0 else jnp.logical_not(low)
                 mine1 = low1 if h % 2 == 0 else jnp.logical_not(low1)
-                row_i = jnp.where(lane == h, jnp.sum(jnp.where(mine, re, 0.0), axis=1, keepdims=True), row_i)
-                col_i = jnp.where(lane == h, jnp.sum(jnp.where(mine, ci, 0.0), axis=1, keepdims=True), col_i)
                 through = jnp.where(
                     lane1 == h, jnp.sum(jnp.where(mine1, th, 0.0), axis=1, keepdims=True), through
                 )
             dx = dtp * jnp.where(low, z[0], z[1]) + bdp * (dtp * ew) + ex_ref[0:1, at] * dyf
-            gch_ref[0:1, at] += jnp.sum(dyf * xp, axis=0, keepdims=True)
+            gch_ref[:, at] += fold(dyf * xp)
             buf[0:Q, at] = dx * ds[:, at]
         daff_b = daff_t.astype(BF16)
         d_bs = nt(xw_s[...], dhb) + nn(daff_b, cb)
@@ -263,12 +268,12 @@
             raw_v = cbuf[8 : 8 + Q, at]
             dk = buf[0:Q, at]
             dv = dk * kw_ref[3:4, at]
-            gcw_ref[4:5, at] += jnp.sum(dk, axis=0, keepdims=True)
-            gcw_ref[3:4, at] += jnp.sum(dk * raw_v, axis=0, keepdims=True)
+            gcw_ref[4, :, at] += fold(dk)
+            gcw_ref[3, :, at] += fold(dk * raw_v)
             for j in range(3):
                 dk = buf[3 - j : 3 - j + Q, at]
                 dv = dv + dk * kw_ref[j : j + 1, at]
-                gcw_ref[j : j + 1, at] += jnp.sum(dk * raw_v, axis=0, keepdims=True)
+                gcw_ref[j, :, at] += fold(dk * raw_v)
             dv_ref[rows, at] = dv.astype(BF16)
         buf[Q : Q + 8, :] = buf[0:8, :]
         between(i0)
@@ -314,7 +319,7 @@
     nf, tok, cot, win, wst, wout, small,
     out_ref, gt_ref, go_ref, gg_ref, gv_ref, gs_ref, small_ref, x_hbm,
     cot_s, nrm_s, wv_s, ws_s, wg_s, wo_s, mix_s, gate_s, mixed_s, st_s, dsh_s,
-    dy_s, dv_s, cotrow_s, part_s, ga_s, gb_s, gc_s,
+    dy_s, dv_s, cotrow_s, part_s, gb_s, gc_s,
     pb0, pb1, pb2, pb3, pb4, lb0, lb1, lb2, lb3, lb4, own0, own1, own2, own3, own4,
     ab0, ab1, az0, az1,
     kw_s, hp_s, ex_s, pre_s, stat_s, stat_own, stat_got,
@@ -322,7 +327,7 @@
     buf, cbuf, dhst, rowp, xw_s, e_s, er_s,
     ls, xs, xr, zs, zr, ms, mr, es, er, bzs, bzr, bxs, bxr, as_, ar, bms, bmr, bes, ber, os_,
 ):
-    x_s, small_s = part_s, snd_s
+    x_s, small_s, ga_s = part_s, snd_s, wo_s
     s = lax.axis_index("seq")
     f = lax.axis_index("fsdp")
     px, py = s ^ 1, s ^ 2
@@ -577,7 +582,9 @@
         gate = gate_s[r, :].astype(F32)
         gated = mixed_s[r, :].astype(F32) * (gate * sigmoid(gate))
         one = jnp.sum(gated * gated, axis=1, keepdims=True)
-        two = jnp.sum(dsh * ex_s[1:2, :] * gated, axis=1, keepdims=True)
+        gained = gated * ex_s[1:2, :]
+        dy_s[r, :] = gained.astype(BF16)
+        two = jnp.sum(dsh * gained, axis=1, keepdims=True)
         stat_own[pl.ds(i, 1), :] = jnp.sum(jnp.where(eye, one, 0.0), axis=0, keepdims=True)
         stat_own[pl.ds(length // 128 + i, 1), :] = jnp.sum(jnp.where(eye, two, 0.0), axis=0, keepdims=True)
         return carry
@@ -586,6 +593,65 @@
     copies = [rcopy(stat_own, stat_got.at[k], es.at[k], er.at[k], {"seq": s ^ k}) for k in range(1, SEQ)]
     for copy in copies:
         copy.start()
+
+    half = D // 2
+    cols = (slice(0, half), slice(half, D))
+    first, second = (px, py), (py, px)
+    ab, az = (ab0, ab1), (az0, az1)
+
+    def chunk(i, a):
+        return part_s.at[pl.ds(i * rows, rows), cols[a]]
+
+    def seq_one(t, a, m):
+        i = (first[a] ^ second[a] ^ s) if m == 0 else first[a]
+        return rcopy(chunk(i, a), ab[t].at[a, m], bxs.at[t, a, m], bxr.at[t, a, m], {"seq": first[a]})
+
+    def seq_two(t, a):
+        return rcopy(az[t].at[a, 0], az[t].at[a, 1], bxs.at[t, a, 2], bxr.at[t, a, 2], {"seq": second[a]})
+
+    def add(*terms):
+        total = terms[0].astype(F32)
+        for term in terms[1:]:
+            total = total + term.astype(F32)
+        return total
+
+    def seq_pass(t):
+        for a in range(2):
+            seq_one(t, a, 0).wait_recv()
+            az[t][a, 0] = add(chunk(second[a], a)[...], ab[t][a, 0]).astype(BF16)
+            seq_two(t, a).start()
+
+    def seq_last(t, out):
+        for a in range(2):
+            seq_one(t, a, 1).wait_recv()
+            seq_two(t, a).wait_recv()
+            out[:, cols[a]] = add(chunk(s, a)[...], ab[t][a, 1], az[t][a, 1])
+
+    def seq_one_sent(t):
+        for a in range(2):
+            seq_one(t, a, 0).wait_send()
+            seq_one(t, a, 1).wait_send()
+
+    x_save.wait()
+
+    def out_part(i, carry):
+        r = pl.ds(pl.multiple_of((s ^ (SEQ - 1 - i)) * rows, rows), rows)
+        part_s[r, :] = nt(dy_s[r, :], wo_s[...]).astype(BF16)
+
+        @pl.when(i == 0)
+        def _():
+            for a in range(2):
+                seq_one(0, a, 0).start()
+
+        @pl.when(i == 2)
+        def _():
+            for a in range(2):
+                seq_one(0, a, 1).start()
+
+        return carry
+
+    lax.fori_loop(0, SEQ, out_part, 0)
+
     for copy in copies:
         copy.wait()
     stat_s[...] = stat_own[...] + stat_got[1] + (stat_got[2] + stat_got[3])
@@ -594,44 +660,6 @@
     st_hop(0, st_own, px).wait_send()
     st_hop(1, st_own, py).wait_send()
     own_row.wait()
-
-    half = D // 2
-    cols = (slice(0, half), slice(half, D))
-    first, second = (px, py), (py, px)
-    ab, az = (ab0, ab1), (az0, az1)
-
-    def chunk(i, a):
-        return part_s.at[pl.ds(i * rows, rows), cols[a]]
-
-    def seq_one(t, a, m):
-        i = (first[a] ^ second[a] ^ s) if m == 0 else first[a]
-        return rcopy(chunk(i, a), ab[t].at[a, m], bxs.at[t, a, m], bxr.at[t, a, m], {"seq": first[a]})
-
-    def seq_two(t, a):
-        return rcopy(az[t].at[a, 0], az[t].at[a, 1], bxs.at[t, a, 2], bxr.at[t, a, 2], {"seq": second[a]})
-
-    def add(*terms):
-        total = terms[0].astype(F32)
-        for term in terms[1:]:
-            total = total + term.astype(F32)
-        return total
-
-    def seq_pass(t):
-        for a in range(2):
-            seq_one(t, a, 0).wait_recv()
-            az[t][a, 0] = add(chunk(second[a], a)[...], ab[t][a, 0]).astype(BF16)
-            seq_two(t, a).start()
-
-    def seq_last(t, out):
-        for a in range(2):
-            seq_one(t, a, 1).wait_recv()
-            seq_two(t, a).wait_recv()
-            out[:, cols[a]] = add(chunk(s, a)[...], ab[t][a, 1], az[t][a, 1])
-
-    def seq_one_sent(t):
-        for a in range(2):
-            seq_one(t, a, 0).wait_send()
-            seq_one(t, a, 1).wait_send()
 
     low_half, high_half = slice(0, W // 2), slice(W // 2, W)
     parts = (ga_s, gb_s, ga_s.at[:, low_half], ga_s.at[:, high_half], gc_s)
@@ -758,7 +786,7 @@
         sg = sigmoid(gate)
         sl = gate * sg
         n1 = mixed * sl * rho
-        gpost_s[0:1, :] += jnp.sum(dsh * n1, axis=0, keepdims=True)
+        gpost_s[...] += fold(dsh * n1)
         d_gated = rho * (dsh * post - n1 * mean)
         mixed_s[r, :] = (n1 * post).astype(BF16)
         dy_s[r, :] = (d_gated * sl).astype(BF16)
@@ -768,30 +796,14 @@
     lax.fori_loop(0, length // 128, gated_norm, 0)
 
     every = slice(0, W)
-    for j in order:
+    for j in order[:2]:
         strip(j, cot_s, mixed_s, every, ga_s, (0,))
-    ends(0, range(nl // 2))
-    x_save.wait()
+    ends(0, range(1))
+    for j in order[2:]:
+        strip(j, cot_s, mixed_s, every, ga_s, (0,))
+    ends(0, range(1, nl // 2))
     x_load = pltpu.make_async_copy(x_hbm, cot_s, ls.at[8])
     x_load.start()
-
-    def out_part(i, carry):
-        r = pl.ds(pl.multiple_of((s ^ (SEQ - 1 - i)) * rows, rows), rows)
-        part_s[r, :] = nt(mixed_s[r, :], wo_s[...]).astype(BF16)
-
-        @pl.when(i == 0)
-        def _():
-            for a in range(2):
-                seq_one(0, a, 0).start()
-
-        @pl.when(i == 2)
-        def _():
-            for a in range(2):
-                seq_one(0, a, 1).start()
-
-        return carry
-
-    lax.fori_loop(0, SEQ, out_part, 0)
 
     def rows_of(t, a):
         return pl.ds((2 * t + a) * rows, rows)
@@ -819,7 +831,7 @@
         part_s[r, :] = dn.astype(BF16)
         x = cot_s[r, :].astype(F32)
         rho = lax.rsqrt(jnp.sum(x * x, axis=1, keepdims=True) * (1.0 / D) + EPS)
-        gpre_s[5:6, :] += jnp.sum(dn * (x * rho), axis=0, keepdims=True)
+        gpre_s[...] += fold(dn * (x * rho))
 
         @pl.when((s ^ j) == 3)
         def _():
@@ -849,7 +861,7 @@
             seq_one_sent(0)
             x_load.wait()
 
-        @pl.when(jnp.logical_or(i == 1, i == 3))
+        @pl.when(jnp.logical_and(lax.rem(i, 2) == 1, i < 2 * SEQ - 1))
         def _():
             dn_chunk(SEQ - 1 - i // 2)
 
@@ -866,15 +878,14 @@
         def _():
             for t in range(2, nl - 1):
                 slot(1, t)
+
+        @pl.when(i == 5)
+        def _():
             close(0)
 
-        @pl.when(i == 5)
+        @pl.when(i == 6)
         def _():
             dn_pass(3)
-
-        @pl.when(i == 6)
-        def _():
-            close(1)
 
     scan_bwd_blocks(
         mix_s.at[:, 0:W], mix_s.at[:, W:CH], mix_s.at[:, CH:VC], dy_s, st_s, kw_s, hp_s, ex_s,
@@ -887,26 +898,30 @@
     ends(2, range(1))
     ends(3, range(1))
     dn_chunk(0)
+    close(1)
     for j in order[2:]:
         strip(j, nrm_s, dv_s, every, ga_s, (2, 3))
     for k in range(1, nl - 1):
         ends(2, (k,))
         ends(3, (k,))
     slot(2, 1)
-    dn_chunk(1)
     slot(3, 1)
     dn_pass(2)
-    relay(0)
     for j in order:
         strip(j, nrm_s, dv_s, slice(W, VC), gc_s, (4,))
     for t in range(2, nl - 1):
         slot(2, t)
+    relay(0)
 
     conv_s[...] = jnp.zeros_like(conv_s)
-    conv_s[:, pl.ds(pl.multiple_of(s * W, 128), W)] = gcw_s[:, 0:W]
-    conv_s[:, INNER:XBC] = gcw_s[:, W:CH]
+    for j in range(5):
+        tap = jnp.sum(gcw_s[j], axis=0, keepdims=True)
+        conv_s[j : j + 1, pl.ds(pl.multiple_of(s * W, 128), W)] = tap[:, 0:W]
+        conv_s[j : j + 1, INNER:XBC] = tap[:, W:CH]
+    gpre_s[5:6, :] = jnp.sum(gpre_s[...], axis=0, keepdims=True)
     post_s[...] = jnp.zeros_like(post_s)
-    post_s[6:7, pl.ds(pl.multiple_of(s * W, 128), W)] = gpost_s[0:1, :]
+    post_s[6:7, pl.ds(pl.multiple_of(s * W, 128), W)] = jnp.sum(gpost_s[...], axis=0, keepdims=True)
+    channels = jnp.sum(gch_s[...], axis=0, keepdims=True)
     lane8 = lax.broadcasted_iota(jnp.int32, (8, 128), 1)
     row8 = lax.broadcasted_iota(jnp.int32, (8, 128), 0)
     skip = jnp.zeros((1, 128), F32)
@@ -914,7 +929,7 @@
     for h in range(HL):
         at = slice(128 * (h // 2), 128 * (h // 2) + 128)
         half_of = (lane1 < HW) if h % 2 == 0 else (lane1 >= HW)
-        skip = jnp.where(lane1 == h, jnp.sum(jnp.where(half_of, gch_s[0:1, at], 0.0), axis=1, keepdims=True), skip)
+        skip = jnp.where(lane1 == h, jnp.sum(jnp.where(half_of, channels[:, at], 0.0), axis=1, keepdims=True), skip)
     heads = [
         pltpu.roll(jnp.where(row8 == 7, jnp.broadcast_to(v, (8, 128)), 0.0), s * HL, 1)
         for v in (ghd_s[0:1, :], ghd_s[1:2, :], skip)
@@ -924,7 +939,7 @@
     for i in range(nf):
         conv = unplace(conv_s, i * (XBC // nf), XBC // nf)
         block = jnp.where(row512 < 5, conv, 0.0)
-        block = block + unplace(gpre_s, i * (D // nf), D // nf)
+        block = block + jnp.where(row512 == 5, unplace(gpre_s, i * (D // nf), D // nf), 0.0)
         block = block + unplace(post_s, i * (INNER // nf), INNER // nf)
         tiles = []
         for v in heads:
@@ -942,21 +957,25 @@
     ends(4, range(nl - 1))
     for t in range(2, nl - 1):
         slot(3, t)
-    relay(1)
+    dn_pass(1)
     dn_pass(0)
     close(2)
-    dn_pass(1)
     close(3)
+    for t in range(1, nl - 1):
+        slot(4, t)
+    relay(1)
 
     for a in range(2):
         seq_one(0, a, 1).wait_recv()
         seq_two(0, a).wait_recv()
-        at = rows_of(0, a)
-        dsh_s[at, :] = add(dsh_s[at, :], cot_s[mine, cols[a]], ab0[a, 1], az0[a, 1])
+        for k in range(rows // 128):
+            one = stat_s[pl.ds(s * (rows // 128) + k, 1), :]
+            rho = lax.rsqrt(jnp.sum(jnp.where(eye, one, 0.0), axis=1, keepdims=True) * (1.0 / INNER) + EPS)
+            part = slice(128 * k, 128 * k + 128)
+            at = pl.ds(a * rows + 128 * k, 128)
+            x = cot_s[pl.ds(pl.multiple_of(s * rows + 128 * k, 128), 128), cols[a]].astype(F32)
+            dsh_s[at, :] = x + rho * add(dsh_s[at, :], ab0[a, 1, part], az0[a, 1, part])
         result(0, a).start()
-
-    for t in range(1, nl - 1):
-        slot(4, t)
 
     total = snd_s[f]
     for k in range(1, nf):
@@ -969,9 +988,9 @@
 
     for k in range(1, SEQ):
         small_share(k).start()
+    close(4)
     relay(2)
     relay(3)
-    close(4)
 
     for a in range(2):
         seq_one(1, a, 1).wait_recv()
@@ -1055,7 +1074,6 @@
             vm((rows, D), BF16),
             vm((length, D), BF16),
             vm((D, W), BF16),
-            vm((D, W), BF16),
             vm((D, VC - W), BF16),
         ]
         + boxes
@@ -1068,7 +1086,7 @@
             vm((2 * length // 128, 128), F32),
             vm((2 * length // 128, 128), F32),
             vm((SEQ, 2 * length // 128, 128), F32),
-            vm((8, CH), F32),
+            vm((5, 8, CH), F32),
             vm((8, W), F32),
             vm((8, 128), F32),
             vm((8, W), F32),

time: 204 us -> 198 us (0.971); the launches traced: 201 us -> 198 us
  Pallas kernels: 195 us -> 192 us
    pallas_call x1, Pallas kernels: 188 us -> 185 us  [mixer(): pl.pallas_call(functools.partial(mixer_kernel, nf), out_shape=[shape((row...]
where the time goes in v3:
time: 198 us
  Pallas kernels  192 us (97%)
  other arithmetic  3.35 us (2%)
    pallas_call x1, Pallas kernels, mixer(): pl.pallas_call(functools.partial(mixer_kernel, nf), out_shape=[shape((row...  185 us
    pallas_call x1, Pallas kernels, finish(): pl.pallas_call(finish_kernel, grid=(SEQ,), out_shape=[shape(out.shape, F3...  7.25 us

profile of v3, /device:TPU:8, one launch (start us, length us, event | category | flops | bytes accessed | tf_op | source)
XLA Modules:
  0.0 198.0 jit_solution(10731010150809530717)
XLA Ops:
  0.6 0.8 convert_add_fusion
  1.4 1.3 pad_add_fusion.small
  2.7 0.9 slice.3
  3.7 0.7 pad.57.wst
  4.3 185.1 %mixer.1 = (f32[256,1536]{1,0:T(8,128)}, f32[256,1536]{1,0:T(8,128)}, bf16[768,768]{1,0:T(8,128)(2,1)}, bf16[768,768]{1,0:T(8,128)(2,1)}, bf16[768,768]{1,0:T(8,...) custom-call(bf16[256,1536]{1,0:T(8,128)(2,1)} %bitcast.21, ...), custom_call_target="tpu_custom_call" | custom-call | tf_op jit(solution)/shard_map/mixer/pallas_call | solution.py:1053
  189.5 7.3 %finish.1 = (f32[256,1536]{1,0:T(8,128)}, f32[256,1536]{1,0:T(8,128)}, f32[192,6448]{1,0:T(8,128)}, f32[192,3072]{1,0:T(8,128)}, f32[4,416]{1,0:T(4,128)}, /*ind...) custom-call(bf16[4,192,768]{2,1,0:T(8,128)(2,1)} %bitcast.17, ...), custom_call_target="tpu_custom_call" | custom-call | tf_op jit(solution)/shard_map/finish/pallas_call | solution.py:1173
  196.7 1.3 reduce
  (1 shorter events, 0.0 us)

commit v4 on v3

--- a/solution.py
+++ b/solution.py
@@ -20,6 +20,7 @@
 HW = INNER // HEADS
 CH = W + 2 * STATE
 VC = CH + 128
+REST = 2 * STATE + HEADS
 Q = 128
 
 F32 = jnp.float32
@@ -316,7 +317,7 @@
 
 
 def mixer_kernel(
-    nf, tok, cot, win, wst, wout, small,
+    nf, tok, cot, win, wout, small,
     out_ref, gt_ref, go_ref, gg_ref, gv_ref, gs_ref, small_ref, x_hbm,
     cot_s, nrm_s, wv_s, ws_s, wg_s, wo_s, mix_s, gate_s, mixed_s, st_s, dsh_s,
     dy_s, dv_s, cotrow_s, part_s, gb_s, gc_s,
@@ -347,7 +348,7 @@
     quarter = n // SEQ
     ins = (
         win.at[:, pl.ds(pl.multiple_of(INNER + s * W, 128), W)],
-        wst.at[pl.ds(pl.multiple_of(s * quarter, 8), quarter)],
+        win.at[pl.ds(pl.multiple_of(s * quarter, 8), quarter), pl.ds(2 * INNER, REST)],
         win.at[:, pl.ds(pl.multiple_of(s * W, 128), W)],
         wout.at[:, pl.ds(pl.multiple_of(s * W, 128), W)],
     )
@@ -469,6 +470,8 @@
         step(0, k)
     own_send(2)
     own_send(3)
+
+    mix_s[:, CH:VC] = jnp.zeros((length, VC - CH), BF16)
 
     own_small.wait()
     for k in range(1, nf):
@@ -534,7 +537,7 @@
 
     def project_state(i, carry):
         r = pl.ds(pl.multiple_of(i * 256, 256), 256)
-        mix_s[r, W:VC] = nn(nrm_s[r, :], ws_s[...].reshape(D, VC - W)).astype(BF16)
+        mix_s[r, W : W + REST] = nn(nrm_s[r, :], ws_s[...].reshape(D, REST)).astype(BF16)
         return carry
 
     lax.fori_loop(0, length // 256, project, 0)
@@ -827,7 +830,7 @@
     def dn_chunk(j):
         r = pl.ds(pl.multiple_of(j * rows, rows), rows)
         dn = nt(gate_s[r, :], wg_s[...]) + nt(dv_s[r, 0:W], wv_s[...])
-        dn = dn + nt(dv_s[r, W:VC], ws_s[...].reshape(D, VC - W))
+        dn = dn + nt(dv_s[r, W : W + REST], ws_s[...].reshape(D, REST))
         part_s[r, :] = dn.astype(BF16)
         x = cot_s[r, :].astype(F32)
         rho = lax.rsqrt(jnp.sum(x * x, axis=1, keepdims=True) * (1.0 / D) + EPS)
@@ -1038,7 +1041,7 @@
         swaps_sent(g)
 
 
-def mixer(nf, tok, cot, win, wst, wout, small):
+def mixer(nf, tok, cot, win, wout, small):
     shape = jax.ShapeDtypeStruct
     vm = pltpu.VMEM
     dma = pltpu.SemaphoreType.DMA
@@ -1055,13 +1058,13 @@
         out_shape=[shape((rows, D), F32)] * 2
         + [shape((SEQ * n, w), BF16) for w in widths]
         + [shape((8, 512), F32), shape((length, D), BF16)],
-        in_specs=[ANY] * 5 + [VMEM],
+        in_specs=[ANY] * 4 + [VMEM],
         out_specs=[ANY] * 6 + [VMEM, ANY],
         scratch_shapes=[
             vm((length, D), BF16),
             vm((length, D), BF16),
             vm((D, W), BF16),
-            vm((nf, SEQ, n // SEQ, VC - W), BF16),
+            vm((nf, SEQ, n // SEQ, REST), BF16),
             vm((D, W), BF16),
             vm((D, W), BF16),
             vm((length, VC), BF16),
@@ -1129,7 +1132,7 @@
         compiler_params=pltpu.CompilerParams(
             collective_id=1, has_side_effects=True, vmem_limit_bytes=67043328
         ),
-    )(tok, cot, win, wst, wout, small)
+    )(tok, cot, win, wout, small)
 
 
 def finish_kernel(
@@ -1152,7 +1155,8 @@
         cw_o[...] = small[0:4, : cw_o.shape[1]]
         cb_o[...] = small[4:5, : cb_o.shape[1]]
         pre_o[...] = small[5:6, : pre_o.shape[1]]
-        post_o[...] = small[6:7, : post_o.shape[1]]
+        for k in range(post_o.shape[0]):
+            post_o[k : k + 1, :] = small[6:7, 128 * k : 128 * k + post_o.shape[1]]
         heads = step_o.shape[1]
         step_o[...] = small[7:8, :heads]
         decay_o[...] = small[7:8, 128 : 128 + heads]
@@ -1169,7 +1173,9 @@
     def whole(*dims):
         return pl.BlockSpec(dims, lambda i: (0,) * len(dims))
 
-    tiny = [(4, XBC // nf), (1, XBC // nf), (1, n), (1, INNER // nf)] + [(1, HEADS // nf)] * 3
+    np_ = INNER // nf
+    post = (np_ // 128, 128) if np_ % 128 == 0 else (1, np_)
+    tiny = [(4, XBC // nf), (1, XBC // nf), (1, n), post] + [(1, HEADS // nf)] * 3
     return pl.pallas_call(
         finish_kernel,
         grid=(SEQ,),
@@ -1215,7 +1221,6 @@
     cot = cotangent.reshape(cotangent.shape[1:])
     win = input_projection_weight
 
-    w_state = jnp.pad(win[:, 2 * INNER :], ((0, 0), (0, VC - W - (win.shape[1] - 2 * INNER))))
     w_out = output_projection_weight.T
 
     flat, at = jnp.zeros((2048,), F32), 0
@@ -1226,7 +1231,7 @@
         at += size
     taps = jnp.pad(conv_weight.T.astype(F32), ((0, 4), (0, 512 - conv_weight.shape[0])))
     small = taps + jnp.pad(flat.reshape(4, 512), ((4, 0), (0, 0)))
-    out, gt, g_out, g_gate, g_val, g_state, small, _ = mixer(nf, tok, cot, win, w_state, w_out, small)
+    out, gt, g_out, g_gate, g_val, g_state, small, _ = mixer(nf, tok, cot, win, w_out, small)
     block_out, grad_tokens, grad_in, grad_out, cw, cb, pre, post, step, decay, skip = finish(
         nf, g_out, g_gate, g_val, g_state, out, gt, small
     )

time: 198 us -> 196 us (0.990)
  no operation moved by 1% of the time
where the time goes in v4:
time: 196 us; the launch traced here: 195 us
  Pallas kernels  192 us (98%)
  other arithmetic  2.07 us (1%)
    pallas_call x1, Pallas kernels, mixer(): pl.pallas_call(functools.partial(mixer_kernel, nf), out_shape=[shape((row...  185 us
    pallas_call x1, Pallas kernels, finish(): pl.pallas_call(finish_kernel, grid=(SEQ,), out_shape=[shape(out.shape, F3...  7.25 us

profile of v4, /device:TPU:8, one launch (start us, length us, event | category | flops | bytes accessed | tf_op | source)
XLA Modules:
  0.0 195.3 jit_solution(16179777342802233967)
XLA Ops:
  0.6 0.8 convert_add_fusion
  1.4 1.3 pad_add_fusion.small
  2.7 185.1 %mixer.1 = (f32[256,1536]{1,0:T(8,128)}, f32[256,1536]{1,0:T(8,128)}, bf16[768,768]{1,0:T(8,128)(2,1)}, bf16[768,768]{1,0:T(8,128)(2,1)}, bf16[768,768]{1,0:T(8,...) custom-call(bf16[256,1536]{1,0:T(8,128)(2,1)} %bitcast.22, ...), custom_call_target="tpu_custom_call" | custom-call | tf_op jit(solution)/shard_map/mixer/pallas_call | solution.py:1056
  187.9 7.3 %finish.1 = (f32[256,1536]{1,0:T(8,128)}, f32[256,1536]{1,0:T(8,128)}, f32[192,6448]{1,0:T(8,128)}, f32[192,3072]{1,0:T(8,128)}, f32[4,416]{1,0:T(4,128)}, /*ind...) custom-call(bf16[4,192,768]{2,1,0:T(8,128)(2,1)} %bitcast.19, ...), custom_call_target="tpu_custom_call" | custom-call | tf_op jit(solution)/shard_map/finish/pallas_call | solution.py:1179
  (1 shorter events, 0.0 us)

commit v5 on v4

--- a/solution.py
+++ b/solution.py
@@ -804,7 +804,7 @@
     ends(0, range(1))
     for j in order[2:]:
         strip(j, cot_s, mixed_s, every, ga_s, (0,))
-    ends(0, range(1, nl // 2))
+    ends(0, range(1, nl - 1))
     x_load = pltpu.make_async_copy(x_hbm, cot_s, ls.at[8])
     x_load.start()
 
@@ -820,9 +820,7 @@
 
     for j in order:
         strip(j, nrm_s, gate_s, every, gb_s, (1,))
-    ends(1, range(nl // 2))
-    ends(0, range(nl // 2, nl - 1))
-    ends(1, range(nl // 2, nl - 1))
+    ends(1, range(nl - 1))
     slot(0, 1)
 
     gpre_s[...] = jnp.zeros_like(gpre_s)
@@ -873,21 +871,18 @@
             for t in range(2, nl - 1):
                 slot(0, t)
 
-        @pl.when(i == 2)
+        @pl.when(i == 3)
+        def _():
+            close(0)
+
+        @pl.when(i == 4)
         def _():
             slot(1, 1)
 
-        @pl.when(i == 4)
+        @pl.when(i == 6)
         def _():
             for t in range(2, nl - 1):
                 slot(1, t)
-
-        @pl.when(i == 5)
-        def _():
-            close(0)
-
-        @pl.when(i == 6)
-        def _():
             dn_pass(3)
 
     scan_bwd_blocks(
@@ -910,11 +905,11 @@
     slot(2, 1)
     slot(3, 1)
     dn_pass(2)
+    relay(0)
     for j in order:
         strip(j, nrm_s, dv_s, slice(W, VC), gc_s, (4,))
     for t in range(2, nl - 1):
         slot(2, t)
-    relay(0)
 
     conv_s[...] = jnp.zeros_like(conv_s)
     for j in range(5):

time: 196 us -> 192 us (0.980); the launches traced: 195 us -> 189 us
  Pallas kernels: 192 us -> 186 us
    pallas_call x1, Pallas kernels: 185 us -> 179 us  [mixer(): pl.pallas_call(functools.partial(mixer_kernel, nf), out_shape=[shape((row...]
where the time goes in v5:
time: 192 us; the launch traced here: 189 us
  Pallas kernels  186 us (97%)
  other arithmetic  2.07 us (1%)
    pallas_call x1, Pallas kernels, mixer(): pl.pallas_call(functools.partial(mixer_kernel, nf), out_shape=[shape((row...  179 us
    pallas_call x1, Pallas kernels, finish(): pl.pallas_call(finish_kernel, grid=(SEQ,), out_shape=[shape(out.shape, F3...  7.25 us

profile of v5, /device:TPU:8, one launch (start us, length us, event | category | flops | bytes accessed | tf_op | source)
XLA Modules:
  0.0 189.0 jit_solution(1366269587797161227)
XLA Ops:
  0.6 0.8 convert_add_fusion
  1.4 1.3 pad_add_fusion.small
  2.7 178.9 %mixer.1 = (f32[256,1536]{1,0:T(8,128)}, f32[256,1536]{1,0:T(8,128)}, bf16[768,768]{1,0:T(8,128)(2,1)}, bf16[768,768]{1,0:T(8,128)(2,1)}, bf16[768,768]{1,0:T(8,...) custom-call(bf16[256,1536]{1,0:T(8,128)(2,1)} %bitcast.22, ...), custom_call_target="tpu_custom_call" | custom-call | tf_op jit(solution)/shard_map/mixer/pallas_call | solution.py:1051
  181.6 7.3 %finish.1 = (f32[256,1536]{1,0:T(8,128)}, f32[256,1536]{1,0:T(8,128)}, f32[192,6448]{1,0:T(8,128)}, f32[192,3072]{1,0:T(8,128)}, f32[4,416]{1,0:T(4,128)}, /*ind...) custom-call(bf16[4,192,768]{2,1,0:T(8,128)(2,1)} %bitcast.19, ...), custom_call_target="tpu_custom_call" | custom-call | tf_op jit(solution)/shard_map/finish/pallas_call | solution.py:1174
  (1 shorter events, 0.0 us)

commit v6 on v5

--- a/solution.py
+++ b/solution.py
@@ -1143,7 +1143,8 @@
         total = total + gs[i].astype(F32)
     rest = gin_o.shape[1] - 2 * INNER
     gin_o[:, 2 * INNER :] = total[:, :rest]
-    gout_o[...] = go[0].astype(F32)
+    for i in range(2):
+        gout_o[:, i * W : i * W + W] = go[i].astype(F32)
 
     @pl.when(pl.program_id(0) == 0)
     def _():
@@ -1161,7 +1162,8 @@
 def finish(nf, go, gg, gv, gs, out, gt, small):
     shape = jax.ShapeDtypeStruct
     n = D // nf
-    step, rows = n // SEQ, out.shape[0] // SEQ
+    steps = SEQ // 2
+    step, rows = n // steps, out.shape[0] // steps
     proj = 2 * INNER + 2 * STATE + HEADS
     go, gg, gv, gs = (g.reshape(SEQ, n, g.shape[1]) for g in (go, gg, gv, gs))
 
@@ -1173,12 +1175,12 @@
     tiny = [(4, XBC // nf), (1, XBC // nf), (1, n), post] + [(1, HEADS // nf)] * 3
     return pl.pallas_call(
         finish_kernel,
-        grid=(SEQ,),
+        grid=(steps,),
         out_shape=[shape(out.shape, F32)] * 2
         + [shape((n, proj), F32), shape((n, INNER), F32)]
         + [shape(dims, F32) for dims in tiny],
         in_specs=[
-            pl.BlockSpec((1, n, W), lambda i: (i, 0, 0)),
+            pl.BlockSpec((2, n, W), lambda i: (i, 0, 0)),
             pl.BlockSpec((SEQ, step, W), lambda i: (0, i, 0)),
             pl.BlockSpec((SEQ, step, W), lambda i: (0, i, 0)),
             pl.BlockSpec((SEQ, step, VC - W), lambda i: (0, i, 0)),
@@ -1190,7 +1192,7 @@
             pl.BlockSpec((rows, D), lambda i: (i, 0)),
             pl.BlockSpec((rows, D), lambda i: (i, 0)),
             pl.BlockSpec((step, proj), lambda i: (i, 0)),
-            pl.BlockSpec((n, W), lambda i: (0, i)),
+            pl.BlockSpec((n, 2 * W), lambda i: (0, i)),
         ]
         + [whole(*dims) for dims in tiny],
         name="finish",

time: 192 us -> 192 us (level)
  no operation moved by 1% of the time
where the time goes in v6:
time: 192 us; the launch traced here: 188 us
  Pallas kernels  185 us (96%)
  other arithmetic  2.07 us (1%)
    pallas_call x1, Pallas kernels, mixer(): pl.pallas_call(functools.partial(mixer_kernel, nf), out_shape=[shape((row...  179 us
    pallas_call x1, Pallas kernels, finish(): pl.pallas_call(finish_kernel, grid=(steps,), out_shape=[shape(out.shape,...  6.38 us

profile of v6, /device:TPU:8, one launch (start us, length us, event | category | flops | bytes accessed | tf_op | source)
XLA Modules:
  0.0 188.2 jit_solution(2014843541778787075)
XLA Ops:
  0.6 0.8 convert_add_fusion
  1.4 1.3 pad_add_fusion.small
  2.7 178.9 %mixer.1 = (f32[256,1536]{1,0:T(8,128)}, f32[256,1536]{1,0:T(8,128)}, bf16[768,768]{1,0:T(8,128)(2,1)}, bf16[768,768]{1,0:T(8,128)(2,1)}, bf16[768,768]{1,0:T(8,...) custom-call(bf16[256,1536]{1,0:T(8,128)(2,1)} %bitcast.22, ...), custom_call_target="tpu_custom_call" | custom-call | tf_op jit(solution)/shard_map/mixer/pallas_call | solution.py:1051
  181.6 6.4 %finish.1 = (f32[256,1536]{1,0:T(8,128)}, f32[256,1536]{1,0:T(8,128)}, f32[192,6448]{1,0:T(8,128)}, f32[192,3072]{1,0:T(8,128)}, f32[4,416]{1,0:T(4,128)}, /*ind...) custom-call(bf16[4,192,768]{2,1,0:T(8,128)(2,1)} %bitcast.19, ...), custom_call_target="tpu_custom_call" | custom-call | tf_op jit(solution)/shard_map/finish/pallas_call | solution.py:1176
  (1 shorter events, 0.0 us)
